TPU v7x, 512 devices: a whole 4x8x8 slice. The times are simulated.
512 devices in a mesh: row: 32 (over y, x), col: 16 (over z, core).
Axes of the slice: x: 4, y: 8, z: 8, core: 2. Of those that a mesh axis runs over, the one named last changes fastest.
Arguments:
- tokens: bfloat16 [24576, 2048], P('row', 'col'), may hold values from -6 to 6
- out_grad: bfloat16 [24576, 2048], P('row', 'col'), may hold values from -3072 to 3072
- counts: int32 [32], P('row'), may hold values from 65 to 768
- block_moves: int32 [16, 3], replicated, may hold values from 0 to 31, as said below
- segment_ids: int32 [24576], P('row'), may hold values from 0 to 767, never falling along the last dimension, each value on 1 to 128 neighbouring positions
- gate_weight: bfloat16 [2048, 8192], P('row', 'col'), may hold values from -0.125 to 0.125
- up_weight: bfloat16 [2048, 8192], P('row', 'col'), may hold values from -0.125 to 0.125
- down_weight: bfloat16 [2048, 8192], P('row', 'col'), may hold values from -0.0625 to 0.0625
Outputs:
- hidden: bfloat16 [16384, 8192], P('row', 'col')
- gate_grad: float32 [2048, 8192], P('row', 'col')
- up_grad: float32 [2048, 8192], P('row', 'col')
- down_grad: float32 [2048, 8192], P('row', 'col')
Inputs may be any that keep to these rules, and one draw needn't show every extreme that they name: `block_moves`: each row is (source rank, destination rank, block index); the block is a valid block of its source; no two rows share both source and destination, nor both source and block; a rank is the source of at most two rows or the destination of at most one, never both; after the moves every rank holds at most 4 valid blocks and some hold exactly 4. `segment_ids`: never falling along the whole array; each document covers 1 to 128 consecutive slots.
All inputs are finite; a program needn't handle non-finite values.
Results may differ from a plain program's by a relative error of at most 0.015.
Values may be sent and summed in bfloat16 or wider, within the bound.
A program may use at most 64 MiB of HBM per device.

v0:
```python
import jax
import jax.numpy as jnp
from jax import lax
from jax.sharding import Mesh
from jax.sharding import PartitionSpec as P

BLOCK = 128
WORK = 4
ROW = ("row_0", "row_1")


def side_by_side(arrays, axis, dim, along):
    both = jnp.concatenate(arrays, axis=along)
    filled, at, outs = (lax.all_gather(both, axis, axis=dim, tiled=True), 0, [])
    for a in arrays:
        outs.append(lax.slice_in_dim(filled, at, at + a.shape[along], axis=along))
        at += a.shape[along]
    return tuple(outs)


def own_rows(terms, axes):
    running = terms.astype(jnp.bfloat16)
    for axis in axes:
        running = lax.psum_scatter(running, axis, scatter_dimension=0, tiled=True)
    return running.astype(jnp.float32)


def local_terms(gate_sum, up_sum, back_sum):
    logistic = jax.nn.sigmoid(gate_sum)
    activated = gate_sum * logistic
    hidden = (activated * up_sum).astype(jnp.bfloat16)
    gate_back = (back_sum * up_sum * logistic * (1.0 + gate_sum * (1.0 - logistic))).astype(
        jnp.bfloat16
    )
    up_back = (back_sum * activated).astype(jnp.bfloat16)
    return (hidden, gate_back, up_back)


def contract(left_side, right_side):
    return lax.dot_general(
        left_side, right_side, (((0,), (0,)), ((), ())), preferred_element_type=jnp.float32
    )


def on_device(
    tokens, out_grad, counts, block_moves, segment_ids, gate_weight, up_weight, down_weight
):
    ranks_all = lax.axis_size(ROW)
    me_rank = lax.axis_index(ROW)
    slot_rows = tokens.shape[0]
    cap_blocks = slot_rows // BLOCK
    feat_cols = tokens.shape[1]
    my_count = counts[0]
    places = jnp.arange(slot_rows, dtype=jnp.int32)
    following = jnp.concatenate([segment_ids[1:], segment_ids[-1:]])
    own_weight = ((places + 1 < my_count) & (following == segment_ids)).astype(jnp.float32)
    source = block_moves[:, 0]
    target = block_moves[:, 1]
    block_id = block_moves[:, 2]
    block_ids = jnp.arange(cap_blocks, dtype=jnp.int32)
    filled = (my_count + BLOCK - 1) // BLOCK
    moved_out = jnp.any(
        (source[None, :] == me_rank) & (block_id[None, :] == block_ids[:, None]), axis=1
    )
    kept_flag = (block_ids < filled) & jnp.logical_not(moved_out)
    arrive = target == me_rank
    flag_bits = jnp.concatenate([kept_flag, arrive]).astype(jnp.int32)
    local_ids = jnp.concatenate([block_ids, cap_blocks + source])
    list_place = jnp.cumsum(flag_bits) - 1
    slot_ids = jnp.arange(WORK, dtype=jnp.int32)
    slot_hit = (flag_bits[:, None] == 1) & (list_place[:, None] == slot_ids[None, :])
    slot_index = jnp.sum(jnp.where(slot_hit, local_ids[:, None] + 1, 0), axis=0) - 1
    peer_ids = jnp.arange(ranks_all, dtype=jnp.int32)
    outgoing = (source[None, :] == me_rank) & (target[None, :] == peer_ids[:, None])
    send_block = jnp.sum(jnp.where(outgoing, block_id[None, :], 0), axis=1)
    send_live = jnp.any(outgoing, axis=1)
    own_tokens = tokens.reshape(cap_blocks, BLOCK, feat_cols)
    own_grad = out_grad.reshape(cap_blocks, BLOCK, feat_cols)
    own_mask = own_weight.astype(jnp.bfloat16).reshape(cap_blocks, BLOCK)

    def outbox(block_rows):
        chosen = jnp.take(block_rows, send_block, axis=0)
        live_rows = send_live.reshape((-1,) + (1,) * (chosen.ndim - 1))
        return jnp.where(live_rows, chosen, jnp.zeros_like(chosen))

    whole_count = jnp.sum(own_weight).astype(jnp.int32)
    count_parts = jnp.broadcast_to(
        jnp.stack([whole_count // 256, whole_count % 256]).astype(jnp.bfloat16)[None, :],
        (ranks_all, 2),
    )
    got_tokens, got_grad, got_mask, got_parts = (
        lax.all_to_all(outbox(own_tokens), ROW, split_axis=0, concat_axis=0, tiled=True),
        lax.all_to_all(outbox(own_grad), ROW, split_axis=0, concat_axis=0, tiled=True),
        lax.all_to_all(outbox(own_mask), ROW, split_axis=0, concat_axis=0, tiled=True),
        lax.all_to_all(count_parts, ROW, split_axis=0, concat_axis=0, tiled=True),
    )
    part_values = got_parts.astype(jnp.float32)
    loss_total = 256.0 * jnp.sum(part_values[:, 0]) + jnp.sum(part_values[:, 1])

    def to_work(pool_rows):
        chosen = jnp.take(pool_rows, jnp.maximum(slot_index, 0), axis=0)
        live_rows = (slot_index >= 0).reshape((-1,) + (1,) * (chosen.ndim - 1))
        return jnp.where(live_rows, chosen, jnp.zeros_like(chosen))

    work_tokens = to_work(jnp.concatenate([own_tokens, got_tokens])).reshape(
        WORK * BLOCK, feat_cols
    )
    work_grad = to_work(jnp.concatenate([own_grad, got_grad])).reshape(WORK * BLOCK, feat_cols)
    work_mask = to_work(jnp.concatenate([own_mask, got_mask])).reshape(WORK * BLOCK)
    work_weight = work_mask.astype(jnp.float32)
    full_tokens, full_grad = side_by_side((work_tokens, work_grad), "col", 1, 0)
    hidden_cols = gate_weight.shape[1]
    gate_piece, up_piece, down_piece = side_by_side(
        (gate_weight, up_weight, down_weight), ROW, 0, 1
    )
    gate_sum = jnp.dot(full_tokens, gate_piece, preferred_element_type=jnp.float32)
    up_sum = jnp.dot(full_tokens, up_piece, preferred_element_type=jnp.float32)
    back_raw = jnp.dot(full_grad, down_piece, preferred_element_type=jnp.float32)
    back_sum = back_raw * work_weight[:, None]
    hidden, gate_back, up_back = local_terms(gate_sum, up_sum, back_sum)
    weighted = full_grad * work_mask[:, None]

    def term_rows(left_side, right_side):
        return contract(left_side, right_side) / loss_total

    joined = own_rows(
        jnp.concatenate(
            [
                term_rows(full_tokens, gate_back),
                term_rows(full_tokens, up_back),
                term_rows(weighted, hidden),
            ],
            axis=1,
        ),
        ROW,
    )
    gate_grad = joined[:, :hidden_cols]
    up_grad = joined[:, hidden_cols : 2 * hidden_cols]
    down_grad = joined[:, 2 * hidden_cols :]
    return (hidden, gate_grad, up_grad, down_grad)


def solution(mesh):
    torus = Mesh(mesh.devices.reshape(8, 4, mesh.shape["col"]), ("row_0", "row_1", "col"))
    return jax.shard_map(
        on_device,
        mesh=torus,
        in_specs=(
            P(ROW, "col"),
            P(ROW, "col"),
            P(ROW),
            P(),
            P(ROW),
            P(ROW, "col"),
            P(ROW, "col"),
            P(ROW, "col"),
        ),
        out_specs=(P(ROW, "col"), P(ROW, "col"), P(ROW, "col"), P(ROW, "col")),
        check_vma=False,
    )
```

profile of v0, /device:TPU:1, one launch (start us, length us, event | category | flops | bytes accessed | tf_op | source)
XLA Modules:
  0.0 370.9 jit_solution(14221137799837593401)
XLA Ops:
  7.2 0.8 add_bitcast_fusion
  8.0 0.8 slice_compare_fusion
  8.9 1.7 gather_fusion.4
  10.6 1.7 gather_fusion.2
  12.3 1.3 select_select_fusion.1
  13.7 36.6 %all_to_all.25 = bf16[32,128,128]{2,1,0:T(8,128)(2,1)S(1)} all-to-all(bf16[32,128,128]{2,1,0:T(8,128)(2,1)S(1)} %get-tuple-element.47), channel_id=1, replica_groups=mesh['row_0'=8,'row_1'=4,'col'=16] {'row_0','row_1'}, dimensions={0} | all-to-all | bytes 2097152 | tf_op jit(solution)/shard_map/all_to_all | solution.py:93
  50.3 6.5 %all-to-all-start = ((bf16[32,128,128]{2,1,0:T(8,128)(2,1)}), bf16[32,128,128]{2,1,0:T(8,128)(2,1)S(1)}, u32[]{:S(2)}, u32[]{:S(2)}) async-start(bf16[32,128,128]{2,1,0:T(8,128)(2,1)} %get-tuple-element.46), calls=%async_computation | async-start | bytes 2097152 | tf_op jit(solution)/shard_map/all_to_all | solution.py:92
  57.5 0.1 fusion.26
  58.1 0.1 add_reduce_fusion
  58.2 0.1 select_reduce_fusion.1
  58.3 1.2 pad_maximum_fusion.2
  59.5 1.9 gather_fusion.5
  61.4 20.8 %all-to-all-done = bf16[32,128,128]{2,1,0:T(8,128)(2,1)S(1)} async-done(((bf16[32,128,128]{2,1,0:T(8,128)(2,1)}), bf16[32,128,128]{2,1,0:T(8,128)(2,1)S(1)}, u32[]{:S(2)}, u32[]{:S(2)}) %all-to-all-start) | async-done | bytes 1048608 | tf_op jit(solution)/shard_map/all_to_all | solution.py:92
  82.2 0.1 pad_maximum_fusion.1
  82.3 0.6 gather_fusion.3
  82.9 0.1 select_select_fusion.3
  83.0 0.7 pad_maximum_fusion.3
  83.8 0.7 pad_maximum_fusion.4
  84.6 0.6 slice.54
  85.2 0.7 fusion.28
  85.9 0.6 convert_reduce_fusion
  87.3 0.6 broadcast_in_dim.133
  87.9 6.8 %all-to-all-start.3 = ((bf16[32,1,2]{2,1,0:T(2,128)(2,1)}), bf16[32,1,2]{2,1,0:T(2,128)(2,1)S(1)}, u32[]{:S(2)}, u32[]{:S(2)}) async-start(bf16[32,1,2]{2,1,0:T(2,128)(2,1)} %broadcast_in_dim.133), calls=%async_computation.3 | async-start | bytes 32768 | tf_op jit(solution)/shard_map/all_to_all | solution.py:95
  94.8 0.6 gather_fusion
  95.4 0.6 copy.39
  96.1 7.2 %all-to-all-done.3 = bf16[32,1,2]{2,1,0:T(2,128)(2,1)S(1)} async-done(((bf16[32,1,2]{2,1,0:T(2,128)(2,1)}), bf16[32,1,2]{2,1,0:T(2,128)(2,1)S(1)}, u32[]{:S(2)}, u32[]{:S(2)}) %all-to-all-start.3) | async-done | bytes 160 | tf_op jit(solution)/shard_map/all_to_all | solution.py:95
  103.3 3.8 %all-to-all-start.2 = ((bf16[32,1,128]{2,1,0:T(2,128)(2,1)}), bf16[32,1,128]{2,1,0:T(2,128)(2,1)S(1)}, u32[]{:S(2)}, u32[]{:S(2)}) async-start(bf16[32,1,128]{2,1,0:T(2,128)(2,1)} %copy.39), calls=%async_computation.2 | async-start | bytes 32768 | tf_op jit(solution)/shard_map/all_to_all | solution.py:94
  107.1 0.2 reduce-scatter.5.cloned.1.call-start
  107.4 0.6 slice_reduce_fusion
  109.4 6.3 %all-to-all-done.2 = bf16[32,1,128]{2,1,0:T(2,128)(2,1)S(1)} async-done(((bf16[32,1,128]{2,1,0:T(2,128)(2,1)}), bf16[32,1,128]{2,1,0:T(2,128)(2,1)S(1)}, u32[]{:S(2)}, u32[]{:S(2)}) %all-to-all-start.2) | async-done | bytes 8224 | tf_op jit(solution)/shard_map/all_to_all | solution.py:94
  115.7 0.6 gather_fusion.1
  116.3 24.1 %all-gather.3.cloned.1.call-done = bf16[1024,2048]{1,0:T(8,128)(2,1)} async-done(((bf16[1024,128]{1,0:T(8,128)(2,1)}), bf16[1024,2048]{1,0:T(8,128)(2,1)}) %all-gather.3.cloned.1.call-update) | async-done | bytes 4194320 | tf_op jit(solution)/shard_map/all_gather | solution.py:14
  140.4 92.8 %all-gather.5.cloned.1.call-done = bf16[2048,1536]{1,0:T(8,128)(2,1)} async-done(((bf16[64,1536]{1,0:T(8,128)(2,1)}), bf16[2048,1536]{1,0:T(8,128)(2,1)}) %all-gather.5.cloned.1.call-update) | async-done | bytes 6291472 | tf_op jit(solution)/shard_map/all_gather | solution.py:14
  233.2 3.6 fusion.4
  236.9 0.4 copy-done.6
  237.3 3.0 fusion.13
  240.3 1.4 multiply_convert_fusion.2
  241.7 1.4 divide_convert_fusion.1
  243.1 1.5 divide_convert_fusion.2
  244.6 1.4 divide_convert_fusion
  246.0 11.3 %pad_maximum_fusion = bf16[2048,1536]{0,1:T(8,128)(2,1)} fusion(bf16[2048,512]{0,1:T(8,128)(2,1)S(1)} %divide_convert_fusion, bf16[2048,512]{0,1:T(8,128)(2,1)S(1)} %divide_convert_fusion.1, bf16[2048,512]{0,1:T(8,128)(2,1)S(1)} %divide_convert_fusion.2), kind=kLoop, calls=%fused_computation.6 | loop fusion | flops 18874368 | bytes 12582912 | tf_op jit(solution)/shard_map/concatenate | solution.py:127
  257.3 76.0 %reduce-scatter.5.cloned.1.call-done = bf16[256,1536]{0,1:T(8,128)(2,1)} async-done(((bf16[2048,1536]{0,1:T(8,128)(2,1)}), bf16[256,1536]{0,1:T(8,128)(2,1)}) %reduce-scatter.5.cloned.1.call-update) | async-done | bytes 786448 | tf_op jit(solution)/shard_map/reduce_scatter | solution.py:24
  333.3 2.3 copy.44
  335.6 25.3 %reduce-scatter.7.cloned.1.call-done = bf16[64,1536]{1,0:T(8,128)(2,1)} async-done(((bf16[256,1536]{1,0:T(8,128)(2,1)}), bf16[64,1536]{1,0:T(8,128)(2,1)}) %reduce-scatter.7.cloned.1.call-update) | async-done | bytes 196624
  360.9 1.1 copy.45
  362.1 0.8 copy.43
  362.9 0.8 copy.42
  363.6 0.8 copy.41
  (51 shorter events, 1.3 us)
Async XLA Ops:
  12.3 46.0 %copy-start = (bf16[768,128]{1,0:T(8,128)(2,1)S(1)}, bf16[768,128]{1,0:T(8,128)(2,1)}, u32[]{:S(2)}) copy-start(bf16[768,128]{1,0:T(8,128)(2,1)} %param.13) | copy-start | bytes 589828
  13.7 68.5 %copy-start.1 = (bf16[768,128]{1,0:T(8,128)(2,1)S(1)}, bf16[768,128]{1,0:T(8,128)(2,1)}, u32[]{:S(2)}) copy-start(bf16[768,128]{1,0:T(8,128)(2,1)} %param.12) | copy-start | bytes 589828
  50.3 33.5 %copy-start.2 = (bf16[64,512]{1,0:T(8,128)(2,1)S(1)}, bf16[64,512]{1,0:T(8,128)(2,1)}, u32[]{:S(2)}) copy-start(bf16[64,512]{1,0:T(8,128)(2,1)} %param.19) | copy-start | bytes 196612
  50.3 33.5 %copy-start.3 = (bf16[64,512]{1,0:T(8,128)(2,1)S(1)}, bf16[64,512]{1,0:T(8,128)(2,1)}, u32[]{:S(2)}) copy-start(bf16[64,512]{1,0:T(8,128)(2,1)} %param.18) | copy-start | bytes 196612
  50.3 33.5 %copy-start.4 = (bf16[64,512]{1,0:T(8,128)(2,1)S(1)}, bf16[64,512]{1,0:T(8,128)(2,1)}, u32[]{:S(2)}) copy-start(bf16[64,512]{1,0:T(8,128)(2,1)} %param.17) | copy-start | bytes 196612
  50.3 31.9 %all-to-all-start = ((bf16[32,128,128]{2,1,0:T(8,128)(2,1)}), bf16[32,128,128]{2,1,0:T(8,128)(2,1)S(1)}, u32[]{:S(2)}, u32[]{:S(2)}) async-start(bf16[32,128,128]{2,1,0:T(8,128)(2,1)} %get-tuple-element.46), calls=%async_computation | async-start | bytes 2097152 | tf_op jit(solution)/shard_map/all_to_all | solution.py:92
  56.8 27.7 %copy-start.5 = (s32[768]{0:T(1024)S(1)}, s32[768]{0:T(1024)}, u32[]{:S(2)}) copy-start(s32[768]{0:T(1024)} %param.16) | copy-start | bytes 9220
  56.8 83.6 %all-gather.3.cloned.1.call-start = ((), (), s32[]{:S(2)}) async-start(), calls=%async_computation.6 | async-start | bytes 4456448 | tf_op jit(solution)/shard_map/all_gather | solution.py:14
  83.7 149.5 %all-gather.5.cloned.1.call-start = ((), (), s32[]{:S(2)}) async-start(), calls=%async_computation.7 | async-start | bytes 6488064 | tf_op jit(solution)/shard_map/all_gather | solution.py:14
  87.9 15.3 %all-to-all-start.3 = ((bf16[32,1,2]{2,1,0:T(2,128)(2,1)}), bf16[32,1,2]{2,1,0:T(2,128)(2,1)S(1)}, u32[]{:S(2)}, u32[]{:S(2)}) async-start(bf16[32,1,2]{2,1,0:T(2,128)(2,1)} %broadcast_in_dim.133), calls=%async_computation.3 | async-start | bytes 32768 | tf_op jit(solution)/shard_map/all_to_all | solution.py:95
  103.3 12.4 %all-to-all-start.2 = ((bf16[32,1,128]{2,1,0:T(2,128)(2,1)}), bf16[32,1,128]{2,1,0:T(2,128)(2,1)S(1)}, u32[]{:S(2)}, u32[]{:S(2)}) async-start(bf16[32,1,128]{2,1,0:T(2,128)(2,1)} %copy.39), calls=%async_computation.2 | async-start | bytes 32768 | tf_op jit(solution)/shard_map/all_to_all | solution.py:94
  107.1 226.2 %reduce-scatter.5.cloned.1.call-start = ((), (), s32[]{:S(2)}) async-start(), calls=%async_computation.8 | async-start | bytes 7077888 | tf_op jit(solution)/shard_map/reduce_scatter | solution.py:24
  233.2 4.1 %copy-start.6 = (bf16[2048,1536]{1,0:T(8,128)(2,1)S(1)}, bf16[2048,1536]{1,0:T(8,128)(2,1)}, u32[]{:S(2)}) copy-start(bf16[2048,1536]{1,0:T(8,128)(2,1)} %all-gather.5.cloned.1.call-done) | copy-start | bytes 18874372
  237.3 3.0 copy-start.7
  241.7 3.0 copy-start.8
  257.3 103.6 %reduce-scatter.7.cloned.1.call-start = ((), (), s32[]{:S(2)}) async-start(), calls=%async_computation.9 | async-start | bytes 983040
Sparse Core Ops, SparseCore 0:
  83.9 56.4 all-gather.2
  143.6 89.6 all-gather.4
  257.4 75.8 reduce-scatter.4
  336.0 24.8 reduce-scatter.6
where the time goes:
time: 373 us; the launch traced here: 371 us
  waiting for transfers between devices  253 us (68%)
  blocking collectives  36.6 us (10%)
  other arithmetic  20 us (5%)
  starting transfers between devices  17.5 us (5%)
  between operations  16.7 us (4%)
  local copies, waits for them, and re-layouts  15.3 us (4%)
  matrix products  12.3 us (3%)
    all_gather x2, waiting for transfers between devices, side_by_side(): filled, at, outs = (lax.all_gather(both, axis, axis=dim, tiled=True), 0, [])  117 us
    reduce_scatter x1, waiting for transfers between devices, own_rows(): running = lax.psum_scatter(running, axis, scatter_dimension=0, tiled=True)  76 us
    all_to_all x1, blocking collectives, on_device(): lax.all_to_all(outbox(own_grad), ROW, split_axis=0, concat_axis=0, tiled=...  36.6 us
    unnamed x5, waiting for transfers between devices  25.3 us
    all_to_all x1, waiting for transfers between devices, on_device(): lax.all_to_all(outbox(own_tokens), ROW, split_axis=0, concat_axis=0, tile...  20.8 us
    concatenate x1, other arithmetic, on_device(): jnp.concatenate([term_rows(full_tokens, gate_back), term_rows(full_tokens...  11.3 us
  transfers between devices with their start and end apart: 7, of which 7 were waited for; matrix products, arithmetic and copies ran while one was open for 3% of the time, Pallas kernels for 0%

commit v1 on v0

v1 whole, which is shorter than its diff:
```python
import jax
import jax.numpy as jnp
from jax import lax
from jax.experimental import pallas as pl
from jax.experimental.pallas import tpu as pltpu
from jax.sharding import Mesh
from jax.sharding import PartitionSpec as P

BLOCK = 128
WORK = 4
CAP = 6
MOVES = 16
NX, NY, NZ = 4, 8, 8
ROWS = 64
HID = 512
COLS = 3 * HID
MAIN = 384
MSG = 4 * BLOCK + 16
YMSG = 2 * BLOCK + 16
MESH = pl.DeviceIdType.MESH
BF16, F32 = jnp.bfloat16, jnp.float32


def pick_kernel(counts, moves, loss, tok, grad, own, outbox, scal):
    y, x = lax.axis_index("y"), lax.axis_index("x")
    me = y * NX + x
    count = counts[0]
    zero, one = jnp.int32(0), jnp.int32(1)
    src = [moves[m, 0] for m in range(MOVES)]
    dst = [moves[m, 1] for m in range(MOVES)]
    blk = [moves[m, 2] for m in range(MOVES)]

    kept = zero
    chosen = [-one] * WORK
    for b in range(CAP):
        moved = zero
        for m in range(MOVES):
            moved = moved | jnp.where((src[m] == me) & (blk[m] == b), one, zero)
        stays = (b * BLOCK < count) & (moved == 0)
        for s in range(WORK):
            chosen[s] = jnp.where(stays & (kept == s), jnp.int32(b), chosen[s])
        kept = kept + jnp.where(stays, one, zero)

    left = zero
    leaving = [-one] * 2
    arrives = zero
    for m in range(MOVES):
        mine = src[m] == me
        for j in range(2):
            leaving[j] = jnp.where(mine & (left == j), blk[m], leaving[j])
        left = left + jnp.where(mine, one, zero)
        arrives = arrives | jnp.where(dst[m] == me, one, zero)

    def fetch(ref, index):
        at = pl.multiple_of(jnp.maximum(index, 0) * BLOCK, BLOCK)
        live = jnp.where(index >= 0, 1.0, 0.0).astype(F32)
        return (ref[pl.ds(at, BLOCK), :].astype(F32) * live).astype(BF16)

    for s in range(WORK):
        own[0, pl.ds(s * BLOCK, BLOCK), :] = fetch(tok, chosen[s])
        own[1, pl.ds(s * BLOCK, BLOCK), :] = fetch(grad, chosen[s])
    for j in range(2):
        outbox[pl.ds(2 * j * BLOCK, BLOCK), :] = fetch(tok, leaving[j])
        outbox[pl.ds((2 * j + 1) * BLOCK, BLOCK), :] = fetch(grad, leaving[j])
    total = loss[0]
    row = lax.broadcasted_iota(jnp.int32, (16, BLOCK), 0)
    parts = jnp.where(row == 2 * x, total // 256, jnp.where(row == 2 * x + 1, total % 256, 0))
    outbox[pl.ds(4 * BLOCK, 16), :] = parts.astype(F32).astype(BF16)

    nth = [zero] * MOVES
    for m in range(MOVES):
        for before in range(m):
            nth[m] = nth[m] + jnp.where(src[before] == src[m], one, zero)
    for d in range(NY):
        at = -one
        for m in range(MOVES):
            hit = (src[m] // NX == y) & (dst[m] == d * NX + x)
            at = jnp.where(hit, (src[m] % NX) * 2 + nth[m], at)
        for i in range(2 * NX):
            scal[d * 2 * NX + i] = jnp.where(at == i, 1.0, 0.0).astype(F32)
    for s in range(WORK):
        scal[2 * NX * NY + s] = jnp.where((arrives == 1) & (kept == s), 1.0, 0.0).astype(F32)


def pick(counts, moves, loss, tok, grad):
    vmem, smem = pl.BlockSpec(memory_space=pltpu.VMEM), pl.BlockSpec(memory_space=pltpu.SMEM)
    return pl.pallas_call(
        pick_kernel,
        out_shape=(
            jax.ShapeDtypeStruct((2, WORK * BLOCK, BLOCK), BF16),
            jax.ShapeDtypeStruct((MSG, BLOCK), BF16),
            jax.ShapeDtypeStruct((128,), F32),
        ),
        in_specs=[smem, smem, smem, vmem, vmem],
        out_specs=(vmem, vmem, smem),
    )(counts, moves, loss, tok, grad)


LENGTH = []


class Graph:
    def __init__(self):
        self.nodes = {}

    def send(self, name, link, size, needs, make):
        self.nodes[name] = ("send", link, size, tuple(needs), make)

    def work(self, name, cost, rank, needs, run):
        self.nodes[name] = ("work", cost, rank, tuple(needs), run)

    def order(self):
        rate, lag = 46.6e3, 2.4
        todo = list(self.nodes)
        done, flying, free, now, steps = set(), [], {}, 0.0, []
        while todo or flying:
            for name in [n for n in todo if self.nodes[n][0] == "send"]:
                _, link, size, needs, _ = self.nodes[name]
                if all(n in done for n in needs):
                    quick = link == "core"
                    begin = max(now, free.get(link, 0.0))
                    free[link] = begin + size / (rate * (12 if quick else 1))
                    flying.append((free[link] + (1.0 if quick else lag), len(steps), name))
                    steps.append(("start", name))
                    todo.remove(name)
            flying.sort()
            if flying and flying[0][0] <= now:
                name = flying.pop(0)[2]
                steps.append(("wait", name))
                done.add(name)
                continue
            ready = [
                (self.nodes[n][2], i, n)
                for i, n in enumerate(todo)
                if self.nodes[n][0] == "work" and all(m in done for m in self.nodes[n][3])
            ]
            if ready:
                name = min(ready)[2]
                steps.append(("run", name))
                now += self.nodes[name][1]
                done.add(name)
                todo.remove(name)
                continue
            if flying:
                now = flying[0][0]
        LENGTH.append(now)
        return steps


def big_kernel(scal, own, outbox, gate, up, down, hidden, gate_out, up_out, down_out,
               w, z, xt, acc, act, tb, slots, xbuf, ysend, yrecv, own3, send_sem, recv_sem, own_sem):
    y, x = lax.axis_index("y"), lax.axis_index("x")
    zz, core = lax.axis_index("z"), lax.axis_index("core")
    size_of = {"x": NX, "y": NY, "z": NZ}
    mine = {"x": x, "y": y, "z": zz}

    def step(axis, by):
        return lax.rem(mine[axis] + (by % size_of[axis]), size_of[axis])

    barrier = pltpu.get_barrier_semaphore()
    peers = [{"x": step("x", d)} for d in range(1, NX)] + [{"y": step("y", d)} for d in range(1, NY)]
    peers += [{"z": step("z", 1)}, {"z": step("z", -1)}, {"core": 1 - core}]
    for peer in peers:
        pl.semaphore_signal(barrier, inc=1, device_id=peer, device_id_type=MESH)

    own_rows = pl.ds(pl.multiple_of((y * NX + x) * ROWS, ROWS), ROWS)
    feature = zz * 2 + core
    local = [
        pltpu.make_async_copy(outbox, xbuf.at[pl.ds(pl.multiple_of(x * MSG, 16), MSG), :], own_sem.at[0]),
        pltpu.make_async_copy(gate, w.at[own_rows, pl.ds(0, HID)], own_sem.at[1]),
        pltpu.make_async_copy(up, w.at[own_rows, pl.ds(HID, HID)], own_sem.at[2]),
        pltpu.make_async_copy(down, w.at[own_rows, pl.ds(2 * HID, HID)], own_sem.at[3]),
        pltpu.make_async_copy(own.at[:, pl.ds(0, MAIN), :], z.at[feature, :, pl.ds(0, MAIN), :], own_sem.at[4]),
        pltpu.make_async_copy(own.at[:, pl.ds(MAIN, BLOCK), :], own3, own_sem.at[5]),
    ]
    for copy in local:
        copy.start()

    graph = Graph()
    index = {}

    def remote(name, link, size, needs, peer, views):
        i = index.setdefault(name, len(index))

        def make(receiver):
            source, target = views(receiver)
            return pltpu.make_async_remote_copy(
                src_ref=source, dst_ref=target, send_sem=send_sem.at[i], recv_sem=recv_sem.at[i],
                device_id=peer, device_id_type=MESH,
            )

        graph.send(name, link, size, needs, make)

    def spread(tag, axis, size, needs, piece):
        n = size_of[axis]
        arrived = {0: list(needs)}
        for hop in range(1, n // 2 + 1):
            for sign in (1, -1):
                part = None if hop < n // 2 else (0 if sign > 0 else 1)
                name = (tag, sign, hop)

                def views(receiver, sign=sign, hop=hop, part=part):
                    ref = piece(step(axis, -sign * (hop if receiver else hop - 1)), part, receiver)
                    return ref, ref

                remote(name, axis + "-+"[sign > 0], size if part is None else size // 2,
                       needs if hop == 1 else [(tag, sign, hop - 1)], {axis: step(axis, sign)}, views)
                arrived.setdefault((sign * hop) % n, []).append(name)
        return arrived

    def gather_sum(tag, axis, size, own_ready, piece, cost, finish):
        n = size_of[axis]
        slot = {}
        for hop in range(n // 2, 0, -1):
            for sign in (1, -1):
                name = (tag, sign, hop)
                part = None if hop < n // 2 else (0 if sign > 0 else 1)
                slot[sign, hop] = ref = slots.at[len(used)]
                used.append(name)
                if part is not None:
                    ref = ref.at[pl.ds(0, 16), :]

                def views(receiver, sign=sign, hop=hop, part=part, ref=ref):
                    return piece(step(axis, sign * hop), part), ref

                needs = own_ready(sign * hop % n) if hop == n // 2 else [("add", tag, sign, hop)]
                remote(name, axis + "-+"[sign > 0], size if part is None else size // 2, needs,
                       {axis: step(axis, sign)}, views)
                if hop > 1:

                    def add(sign=sign, hop=hop, part=part, ref=ref):
                        into = piece(step(axis, sign * (hop - 1)), part)
                        into[...] = (into[...].astype(F32) + ref[...].astype(F32)).astype(BF16)

                    graph.work(("add", tag, sign, hop - 1), cost, 0,
                               [name] + own_ready(sign * (hop - 1) % n), add)

        def fin():
            finish(piece(mine[axis], None), slot[1, 1], slot[-1, 1])

        graph.work(("fin", tag), 1.5 * cost, 0, [(tag, 1, 1), (tag, -1, 1)] + own_ready(0), fin)

    used = []

    for d in (1, 3, 2):
        def views(receiver, d=d):
            rows = pl.ds(pl.multiple_of((step("x", -d) if receiver else x) * MSG, 16), MSG)
            return xbuf.at[rows, :], xbuf.at[rows, :]
        remote(("mx", d), "x-" if d == 3 else "x+", MSG * BLOCK * 2 * (2 if d == 2 else 1), [],
               {"x": step("x", d)}, views)

    def select():
        counts_rows = sum(xbuf[pl.ds(i * MSG + 4 * BLOCK, 16), :].astype(F32) for i in range(NX)).astype(BF16)
        for d in range(NY):
            chosen = None
            for i in range(2 * NX):
                block = xbuf[pl.ds(i // 2 * MSG + i % 2 * 2 * BLOCK, 2 * BLOCK), :]
                term = block * scal[d * 2 * NX + i].astype(BF16)
                chosen = term if chosen is None else chosen + term
            ysend[d, pl.ds(0, 2 * BLOCK), :] = chosen
            ysend[d, pl.ds(2 * BLOCK, 16), :] = counts_rows

    graph.work("select", 0.8, 0, [("mx", d) for d in (1, 2, 3)], select)
    for d in (1, 7, 2, 6, 3, 5, 4):
        def views(receiver, d=d):
            if receiver:
                return ysend.at[y], yrecv.at[step("y", -d)]
            return ysend.at[step("y", d)], yrecv.at[y]
        remote(("my", d), "y-" if d > 4 else "y+", YMSG * BLOCK * 2 * min(d, 8 - d), ["select"],
               {"y": step("y", d)}, views)

    def merge():
        total = ysend[y].astype(F32)
        for d in range(1, NY):
            total = total + yrecv[step("y", d)].astype(F32)
        for t in range(2):
            z[feature, t, pl.ds(MAIN, BLOCK), :] = (
                total[t * BLOCK : (t + 1) * BLOCK] + own3[t].astype(F32)
            ).astype(BF16)

    graph.work("merge", 0.6, 0, [("my", d) for d in range(1, NY)], merge)

    def loss_total():
        counts_rows = ysend[y, pl.ds(2 * BLOCK, 16), :].astype(F32)
        for d in range(1, NY):
            counts_rows = counts_rows + yrecv[step("y", d), pl.ds(2 * BLOCK, 16), :].astype(F32)
        row = lax.broadcasted_iota(jnp.int32, (16, BLOCK), 0)
        parts = jnp.where(row % 2 == 0, 256.0 * counts_rows, counts_rows)
        return jnp.sum(parts, axis=0, keepdims=True)[:, 0:1]

    def shard(ref, at_y, at_x, base, part):
        first = pl.multiple_of((at_y * NX + at_x) * ROWS + base + (16 if part else 0), 16)
        return ref.at[pl.ds(first, 32 if part is None else 16), :]

    whole = 32 * COLS * 2
    ax = spread("ax", "x", whole, [], lambda o, part, r: shard(w, y, o, 0, part))
    by = spread("by", "y", whole, [], lambda o, part, r: shard(w, o, x, 32, part))
    ay, bx = {}, {}
    for e in ax:
        ay[e] = spread(("ay", e), "y", whole, ax[e], lambda o, part, r, e=e: shard(w, o, step("x", -e), 0, part))
    for f in by:
        bx[f] = spread(("bx", f), "x", whole, by[f], lambda o, part, r, f=f: shard(w, step("y", -f), o, 32, part))

    token_needs = []
    for tag, lo, rows, needs in (("zm", 0, MAIN, []), ("zl", MAIN, BLOCK, ["merge"])):
        def cut(at, part, lo=lo, rows=rows):
            if part is None:
                return z.at[at, :, pl.ds(lo, rows), :]
            return z.at[at, part, pl.ds(lo, rows), :]

        bytes_all = 2 * rows * BLOCK * 2
        arrived = spread(tag, "z", bytes_all, needs, lambda o, part, r, cut=cut: cut(o * 2 + core, part))
        for g, names in arrived.items():
            for i, name in enumerate(names if g else [None]):
                part = i if g == NZ // 2 else None

                def views(receiver, g=g, part=part, cut=cut):
                    ref = cut(step("z", -g) * 2 + (1 - core if receiver else core), part)
                    return ref, ref

                remote(("core", tag, g, i), "core", bytes_all if part is None else bytes_all // 2,
                       [name] if g else needs, {"core": 1 - core}, views)
                token_needs.append(("core", tag, g, i))
        token_needs += [name for names in arrived.values() for name in names]

    first = [True]

    def forward(f):
        start = first[0]
        first[0] = False
        at = step("y", -f)
        rows = pl.ds(pl.multiple_of(at * 256, 256), 256)
        for t, lo, hi in ((0, 0, 4), (1, 4, 6)):
            left = jnp.concatenate([z[at * 2, t], z[at * 2 + 1, t]], axis=1)

            def tile(n, _, left=left):
                cols = pl.ds(pl.multiple_of(n * 256, 256), 256)
                new = jnp.dot(left, w[rows, cols], preferred_element_type=F32)
                acc[:, cols] = new if start else acc[:, cols] + new
                return 0

            lax.fori_loop(lo, hi, tile, 0)

    for f in range(NY):
        needs = token_needs + [n for e in ay for n in ay[e][f]] + [n for e in bx[f] for n in bx[f][e]]
        graph.work(("fwd", f), 1.0, 2, needs, lambda f=f: forward(f))

    def turn(c):
        for t in range(2):
            xt[t, pl.ds(c * BLOCK, BLOCK), :] = z[c, t].T

    for c in range(2 * NZ):
        graph.work(("turn", c), 0.3, 3, token_needs, lambda c=c: turn(c))

    def pointwise():
        def rows_of(i, _):
            rows = pl.ds(pl.multiple_of(i * 64, 64), 64)
            g, u, b = acc[rows, 0:HID], acc[rows, HID : 2 * HID], acc[rows, 2 * HID : COLS]
            logistic = jax.nn.sigmoid(g)
            activated = g * logistic
            act[rows, 0:HID] = (b * u * logistic * (1.0 + g * (1.0 - logistic))).astype(BF16)
            act[rows, HID : 2 * HID] = (b * activated).astype(BF16)
            act[rows, 2 * HID : COLS] = (activated * u).astype(BF16)
            return 0

        lax.fori_loop(0, 8, rows_of, 0)

    graph.work("pointwise", 3.0, 2, [("fwd", f) for f in range(NY)] + [("turn", c) for c in range(2 * NZ)], pointwise)

    def store_hidden():
        last = act[pl.ds(MAIN, BLOCK), 2 * HID : COLS]
        stays = 1.0 - (scal[64] + scal[65] + scal[66])
        for s in range(WORK - 1):
            at = pl.ds(s * BLOCK, BLOCK)
            hidden[at, :] = act[at, 2 * HID : COLS] + last * scal[64 + s].astype(BF16)
        hidden[pl.ds(MAIN, BLOCK), :] = last * stays.astype(BF16)

    graph.work("hidden", 0.5, 9, ["pointwise"], store_hidden)

    def backward(j):
        rows = pl.ds(pl.multiple_of(step("y", j) * 256, 256), 256)
        for t, lo, hi in ((0, 0, 4), (1, 4, 6)):
            def tile(n, _, t=t):
                cols = pl.ds(pl.multiple_of(n * 256, 256), 256)
                tb[rows, cols] = jnp.dot(xt[t, rows, :], act[:, cols], preferred_element_type=F32).astype(BF16)
                return 0

            lax.fori_loop(lo, hi, tile, 0)

    for i, j in enumerate((4, 5, 3, 6, 2, 7, 1, 0)):
        graph.work(("bwd", j), 1.0, 1 + i, ["pointwise"], lambda j=j: backward(j))

    def plain(own_ref, one, other):
        own_ref[...] = (own_ref[...].astype(F32) + one[...].astype(F32) + other[...].astype(F32)).astype(BF16)

    def final(base):
        def run(own_ref, one, other):
            total = loss_total()
            for i, out in enumerate((gate_out, up_out, down_out)):
                cols = pl.ds(i * HID, HID)
                sums = own_ref[:, cols].astype(F32) + one[:, cols].astype(F32) + other[:, cols].astype(F32)
                out[pl.ds(base, 32), :] = sums / total
        return run

    for e in range(NX):
        gather_sum(("say", e), "y", whole, lambda j: [("bwd", j)],
                   lambda o, part, e=e: shard(tb, o, step("x", e), 0, part), 0.15, plain)
    for f in (4, 5, 3, 6, 2, 7, 1, 0):
        gather_sum(("sbx", f), "x", whole, lambda j, f=f: [("bwd", f)],
                   lambda o, part, f=f: shard(tb, step("y", f), o, 32, part), 0.15, plain)
    gather_sum("sax", "x", whole, lambda j: [("fin", ("say", j))],
               lambda o, part: shard(tb, y, o, 0, part), 0.15, final(0))
    gather_sum("sby", "y", whole, lambda j: [("fin", ("sbx", j))],
               lambda o, part: shard(tb, o, x, 32, part), 0.15, final(32))

    pl.semaphore_wait(barrier, len(peers))
    for copy in local:
        copy.wait()
    copies = {}
    for kind, name in graph.order():
        if kind == "run":
            graph.nodes[name][4]()
        elif kind == "start":
            copies[name] = graph.nodes[name][4](False)
            copies[name].start()
        else:
            graph.nodes[name][4](True).wait_recv()
    for copy in copies.values():
        copy.wait_send()


SLOTS = 76
SENDS = 206


def big(scal, own, outbox, gate, up, down):
    vmem, smem = pl.BlockSpec(memory_space=pltpu.VMEM), pl.BlockSpec(memory_space=pltpu.SMEM)
    anyw = pl.BlockSpec(memory_space=pl.ANY)
    grad = jax.ShapeDtypeStruct((ROWS, HID), F32)
    rows = WORK * BLOCK
    return pl.pallas_call(
        big_kernel,
        out_shape=(jax.ShapeDtypeStruct((rows, HID), BF16), grad, grad, grad),
        in_specs=[smem] + [anyw] * 5,
        out_specs=(vmem,) * 4,
        scratch_shapes=[
            pltpu.VMEM((NX * NY * ROWS, COLS), BF16),
            pltpu.VMEM((2 * NZ, 2, rows, BLOCK), BF16),
            pltpu.VMEM((2, 2 * NZ * BLOCK, rows), BF16),
            pltpu.VMEM((rows, COLS), F32),
            pltpu.VMEM((rows, COLS), BF16),
            pltpu.VMEM((NX * NY * ROWS, COLS), BF16),
            pltpu.VMEM((SLOTS, 32, COLS), BF16),
            pltpu.VMEM((NX * MSG, BLOCK), BF16),
            pltpu.VMEM((NY, YMSG, BLOCK), BF16),
            pltpu.VMEM((NY, YMSG, BLOCK), BF16),
            pltpu.VMEM((2, BLOCK, BLOCK), BF16),
            pltpu.SemaphoreType.DMA((SENDS,)),
            pltpu.SemaphoreType.DMA((SENDS,)),
            pltpu.SemaphoreType.DMA((6,)),
        ],
        compiler_params=pltpu.CompilerParams(
            collective_id=0, has_side_effects=True, vmem_limit_bytes=60 * 1024 * 1024
        ),
    )(scal, own, outbox, gate, up, down)


def on_device(tokens, out_grad, counts, block_moves, segment_ids, gate, up, down):
    places = jnp.arange(tokens.shape[0], dtype=jnp.int32)
    following = jnp.concatenate([segment_ids[1:], segment_ids[-1:]])
    keep = (places + 1 < counts[0]) & (following == segment_ids)
    loss = jnp.sum(keep.astype(jnp.int32)).reshape(1)
    weighted = out_grad * keep.astype(BF16)[:, None]
    own, outbox, scal = pick(counts, block_moves, loss, tokens, weighted)
    return big(scal, own, outbox, gate, up, down)


def solution(mesh):
    torus = Mesh(mesh.devices.reshape(NY, NX, NZ, 2), ("y", "x", "z", "core"))
    row, col = ("y", "x"), ("z", "core")
    return jax.shard_map(
        on_device,
        mesh=torus,
        in_specs=(P(row, col), P(row, col), P(row), P(), P(row), P(row, col), P(row, col), P(row, col)),
        out_specs=(P(row, col),) * 4,
        check_vma=False,
    )
```

time: 373 us -> 145 us (0.39)
  waiting for transfers between devices: 253 us -> 0 us
  Pallas kernels: 0 us -> 133 us
  blocking collectives: 36.6 us -> 0 us
  starting transfers between devices: 17.5 us -> 0 us
  other arithmetic: 20 us -> 3.12 us
  between operations: 16.7 us -> 1.33 us
  matrix products: 12.3 us -> 0 us
  local copies, waits for them, and re-layouts: 15.3 us -> 7.17 us
    pallas_call x0 -> x2, Pallas kernels: none -> 133 us  [the longest x1 130 us: big(): pl.pallas_call(big_kernel, out_shape=(jax.ShapeDtypeStruct((rows, HID), B...]
    all_gather x2 -> x0, waiting for transfers between devices: 117 us -> none  [side_by_side(): filled, at, outs = (lax.all_gather(both, axis, axis=dim, tiled=True), 0, [])]
    reduce_scatter x1 -> x0, waiting for transfers between devices: 76 us -> none  [own_rows(): running = lax.psum_scatter(running, axis, scatter_dimension=0, tiled=True)]
    all_to_all x1 -> x0, blocking collectives: 36.6 us -> none  [on_device(): lax.all_to_all(outbox(own_grad), ROW, split_axis=0, concat_axis=0, tiled=...]
    all_to_all x3 -> x0, waiting for transfers between devices: 34.3 us -> none  [the longest x1 20.8 us: on_device(): lax.all_to_all(outbox(own_tokens), ROW, split_axis=0, concat_axis=0, tile...]
    unnamed x5 -> x0, waiting for transfers between devices: 25.3 us -> none
    all_to_all x3 -> x0, starting transfers between devices: 17.1 us -> none  [the longest x1 6.8 us: on_device(): lax.all_to_all(count_parts, ROW, split_axis=0, concat_axis=0, tiled=True)]
    concatenate x8 -> x0, other arithmetic: 14.8 us -> none  [the longest x1 11.3 us: on_device(): jnp.concatenate([term_rows(full_tokens, gate_back), term_rows(full_tokens...]
  transfers between devices with their start and end apart: 7 -> 0, of which waited for: 7 -> 0; matrix products, arithmetic and copies ran while one was open for 3% -> 0% of each run, Pallas kernels for 0% -> 0%
where the time goes in v1:
time: 145 us
  Pallas kernels  133 us (92%)
  local copies, waits for them, and re-layouts  7.17 us (5%)
  other arithmetic  3.12 us (2%)
    pallas_call x1, Pallas kernels, big(): pl.pallas_call(big_kernel, out_shape=(jax.ShapeDtypeStruct((rows, HID), B...  130 us
    unnamed x15, local copies, waits for them, and re-layouts  5.83 us
    pallas_call x1, Pallas kernels, pick(): pl.pallas_call(pick_kernel, out_shape=(jax.ShapeDtypeStruct((2, WORK * BL...  3.27 us

profile of v1, /device:TPU:1, one launch (start us, length us, event | category | flops | bytes accessed | tf_op | source)
XLA Modules:
  0.0 144.6 jit_solution(3378585247388959093)
XLA Ops:
  0.6 0.0 copy-start.3
  1.3 1.3 slice.7
  2.6 0.0 copy-done.3
  2.6 0.1 slice.6
  2.6 0.7 fusion.1
  3.4 0.6 convert_reduce_fusion
  4.0 0.0 copy-start.4
  4.0 0.7 copy-done.4
  4.7 0.7 copy.12.moves
  5.4 1.8 %broadcast_multiply_fusion.grad = bf16[768,128]{1,0:T(8,128)(2,1)} fusion(bf16[768,128]{1,0:T(8,128)(2,1)} %param.9, bf16[768]{0:T(1024)(128)(2,1)S(1)} %get-tuple-element.10), kind=kLoop, calls=%fused_computation | loop fusion | flops 98304 | bytes 394752 | tf_op jit(solution)/shard_map/mul | solution.py:473
  7.1 3.3 %shard_map.111 = (bf16[2,512,128]{2,1,0:T(8,128)(2,1)}, bf16[528,128]{1,0:T(8,128)(2,1)}, f32[128]{0:T(128)}) custom-call(s32[1]{0:T(128)} %copy.17.counts, s32[16,3]{1,0:T(8,128)} %copy.12.moves, s32[1]{0:T(128)} %bitcast.1.loss, bf16[768,128]{1,0:T(8,128)(2,1)} %tok.1, bf16[768,128]{1,0:T(8,128)(2,1)} %broadcast_multiply_fusion.grad), custom_call_target="tpu_custom_call" | custom-call | tf_op jit(solution)/shard_map/pallas_call | solution.py:87
  10.4 129.7 %shard_map.112 = (bf16[512,512]{1,0:T(8,128)(2,1)}, f32[64,512]{1,0:T(8,128)}, f32[64,512]{1,0:T(8,128)}, f32[64,512]{1,0:T(8,128)}) custom-call(f32[128]{0:T(128)} %get-tuple-element.7.scal, bf16[2,512,128]{2,1,0:T(8,128)(2,1)} %get-tuple-element.8.own, bf16[528,128]{1,0:T(8,128)(2,1)} %get-tuple-element.9.outbox, bf16[64,512]{1,0:T(8,128)(2,1)} %gate.1, ...), custom_call_target="tpu_custom_call" | custom-call | tf_op jit(solution)/shard_map/pallas_call | solution.py:441
  140.1 0.0 copy-start.2
  140.1 1.9 %copy.18 = bf16[512,512]{1,0:T(8,128)(2,1)} copy(bf16[512,512]{1,0:T(8,128)(2,1)} %get-tuple-element.16) | data formatting | bytes 1048576
  142.0 0.0 copy-done.2
  142.0 0.0 copy-start.1
  142.0 0.7 copy.19
  142.7 0.3 copy-done.1
  143.0 0.0 copy-start
  143.0 0.7 copy.20
  143.6 0.3 copy-done
  143.9 0.7 copy.21
Async XLA Ops:
  0.6 1.9 %copy-start.3 = (s32[768]{0:T(1024)S(1)}, s32[768]{0:T(1024)}, u32[]{:S(2)}) copy-start(s32[768]{0:T(1024)} %param.12) | copy-start | bytes 9220
  4.0 0.7 copy-start.4
  140.1 1.9 %copy-start.2 = (f32[64,512]{1,0:T(8,128)S(1)}, f32[64,512]{1,0:T(8,128)}, u32[]{:S(2)}) copy-start(f32[64,512]{1,0:T(8,128)} %get-tuple-element.17) | copy-start | bytes 393220
  142.0 1.0 copy-start.1
  143.0 1.0 copy-start

commit v2 on v1

v2 whole, which is shorter than its diff:
```python
import jax
import jax.numpy as jnp
from jax import lax
from jax.experimental import pallas as pl
from jax.experimental.pallas import tpu as pltpu
from jax.sharding import Mesh
from jax.sharding import PartitionSpec as P

BLOCK = 128
WORK = 4
CAP = 6
MOVES = 16
NX, NY, NZ = 4, 8, 8
ROWS = 64
HID = 512
COLS = 3 * HID
MAIN = 384
MSG = 4 * BLOCK + 16
YMSG = 2 * BLOCK + 16
CUT = {"a": (0, 640), "b": (640, 896)}
MESH = pl.DeviceIdType.MESH
BF16, F32 = jnp.bfloat16, jnp.float32


def choose(y, x, counts, moves):
    me = y * NX + x
    count = counts[0]
    zero, one = jnp.int32(0), jnp.int32(1)
    src = [moves[0, m] for m in range(MOVES)]
    dst = [moves[1, m] for m in range(MOVES)]
    blk = [moves[2, m] for m in range(MOVES)]
    src_y = [lax.div(v, jnp.int32(NX)) for v in src]
    src_x = [v - NX * w for v, w in zip(src, src_y)]

    def factor(flag):
        return jnp.where(flag, 1.0, 0.0).astype(F32)

    left = zero
    leaving = [-one] * 2
    arrives = zero
    for m in range(MOVES):
        mine = src[m] == me
        for j in range(2):
            leaving[j] = jnp.where(mine & (left == j), blk[m], leaving[j])
        left = left + jnp.where(mine, one, zero)
        arrives = arrives | jnp.where(dst[m] == me, one, zero)
    kept = zero
    chosen = [-one] * WORK
    for b in range(CAP):
        stays = (b * BLOCK < count) & (leaving[0] != b) & (leaving[1] != b)
        for s in range(WORK):
            chosen[s] = jnp.where(stays & (kept == s), jnp.int32(b), chosen[s])
        kept = kept + jnp.where(stays, one, zero)
    stay = [[factor(chosen[s] == b) for b in range(CAP)] for s in range(WORK)]
    leave = [[factor(leaving[j] == b) for b in range(CAP)] for j in range(2)]

    second = [zero] * MOVES
    for m in range(MOVES):
        for before in range(m):
            second[m] = second[m] | jnp.where(src[before] == src[m], one, zero)
    route = []
    for d in range(NY):
        at = -one
        for m in range(MOVES):
            hit = (src_y[m] == y) & (dst[m] == d * NX + x)
            at = jnp.where(hit, src_x[m] * 2 + second[m], at)
        route.append([factor(at == i) for i in range(2 * NX)])
    slot = [factor((arrives == 1) & (kept == s)) for s in range(WORK)]
    return stay, leave, route, slot


def blend(factors, blocks):
    total = None
    for f, block in zip(factors, blocks):
        term = block * f.astype(BF16)
        total = term if total is None else total + term
    return total


TIMES = {}


class Graph:
    def __init__(self):
        self.nodes = {}

    def send(self, name, link, size, needs, make):
        self.nodes[name] = ("send", link, size, tuple(needs), make)

    def work(self, name, cost, rank, needs, run):
        self.nodes[name] = ("work", cost, rank, tuple(needs), run)

    def order(self):
        rate, lag = 46.6e3, 2.2
        nodes = self.nodes
        after = {n: [] for n in nodes}
        for n, node in nodes.items():
            for m in node[3]:
                after[m].append(n)
        below = {}

        def span(n):
            if nodes[n][0] == "work":
                return nodes[n][1]
            quick = nodes[n][1] == "core"
            return nodes[n][2] / (rate * (12 if quick else 1)) + (1.0 if quick else lag)

        def urgency(n):
            if n not in below:
                below[n] = span(n) + max([urgency(m) for m in after[n]], default=0.0)
            return below[n]

        todo = sorted(nodes, key=lambda n: -urgency(n))
        done, flying, free, now, steps = set(), [], {}, 0.0, []
        while todo or flying:
            ahead = 2.5 if ("fin", "my") in done else 0.6
            for name in [n for n in todo if nodes[n][0] == "send"]:
                _, link, size, needs, _ = nodes[name]
                quick = link == "core"
                if all(n in done for n in needs) and free.get(link, 0.0) - now < ahead:
                    begin = max(now, free.get(link, 0.0))
                    free[link] = begin + size / (rate * (12 if quick else 1))
                    flying.append((free[link] + (1.0 if quick else lag), len(steps), name))
                    steps.append(("start", name))
                    todo.remove(name)
            flying.sort()
            if flying and flying[0][0] <= now:
                name = flying.pop(0)[2]
                steps.append(("wait", name))
                done.add(name)
                continue
            ready = [n for n in todo if nodes[n][0] == "work" and all(m in done for m in nodes[n][3])]
            if ready:
                steps.append(("run", ready[0]))
                now += nodes[ready[0]][1]
                TIMES[ready[0]] = now
                done.add(ready[0])
                todo.remove(ready[0])
                continue
            if flying:
                now = flying[0][0]
        TIMES["end"] = now
        return steps


def big_kernel(counts, moves, seg, tok, grad, gate, up, down, hidden_out, sums_hbm,
               w, z, xt, acc, act, tb, slots_a, slots_b, slots_m, xbuf, ysend, own3, tokv, gradv, marks, hidden, sums_out,
               send_sem, recv_sem, own_sem):
    y, x = lax.axis_index("y"), lax.axis_index("x")
    zz, core = lax.axis_index("z"), lax.axis_index("core")
    size_of = {"x": NX, "y": NY, "z": NZ}
    mine = {"x": x, "y": y, "z": zz}

    def step(axis, by):
        return lax.rem(mine[axis] + (by % size_of[axis]), size_of[axis])

    barrier = pltpu.get_barrier_semaphore()
    peers = [{axis: step(axis, by)} for axis in ("x", "y", "z") for by in (1, -1)] + [{"core": 1 - core}]
    for peer in peers:
        pl.semaphore_signal(barrier, inc=1, device_id=peer, device_id_type=MESH)

    own_rows = pl.ds(pl.multiple_of((y * NX + x) * ROWS, ROWS), ROWS)
    feature = zz * 2 + core
    local = [
        pltpu.make_async_copy(gate, w.at[own_rows, pl.ds(0, HID)], own_sem.at[0]),
        pltpu.make_async_copy(up, w.at[own_rows, pl.ds(HID, HID)], own_sem.at[1]),
        pltpu.make_async_copy(down, w.at[own_rows, pl.ds(2 * HID, HID)], own_sem.at[2]),
    ]
    local_rows = [
        pltpu.make_async_copy(tok, tokv, own_sem.at[3]),
        pltpu.make_async_copy(grad, gradv, own_sem.at[4]),
    ]
    for copy in local + local_rows:
        copy.start()
    stay, leave, route, slot_of = choose(y, x, counts, moves)

    graph = Graph()
    index = {}

    def remote(name, link, size, needs, peer, views):
        i = index.setdefault(name, len(index))

        def make(receiver):
            source, target = views(receiver)
            return pltpu.make_async_remote_copy(
                src_ref=source, dst_ref=target, send_sem=send_sem.at[i], recv_sem=recv_sem.at[i],
                device_id=peer, device_id_type=MESH,
            )

        graph.send(name, link, size, needs, make)

    def spread(tag, axis, size, needs, piece):
        n = size_of[axis]
        arrived = {0: list(needs)}
        for hop in range(1, n // 2 + 1):
            for sign in (1, -1):
                part = None if hop < n // 2 else (0 if sign > 0 else 1)
                name = (tag, sign, hop)

                def views(receiver, sign=sign, hop=hop, part=part):
                    ref = piece(step(axis, -sign * (hop if receiver else hop - 1)), part, receiver)
                    return ref, ref

                remote(name, axis + "-+"[sign > 0], size if part is None else size // 2,
                       needs if hop == 1 else [(tag, sign, hop - 1)], {axis: step(axis, sign)}, views)
                arrived.setdefault((sign * hop) % n, []).append(name)
        return arrived

    def gather_sum(tag, axis, size, own_ready, piece, cost, finish, pool, halves):
        n = size_of[axis]
        slot = {}
        slots, used = pool
        for hop in range(n // 2, 0, -1):
            for sign in (1, -1):
                name = (tag, sign, hop)
                part = None if hop < n // 2 else (0 if sign > 0 else 1)
                slot[sign, hop] = ref = slots.at[len(used)]
                used.append(name)
                if part is not None:
                    ref = ref.at[halves[part], :]

                def views(receiver, sign=sign, hop=hop, part=part, ref=ref):
                    return piece(step(axis, sign * hop), part), ref

                needs = own_ready(sign * hop % n) if hop == n // 2 else [("add", tag, sign, hop)]
                remote(name, axis + "-+"[sign > 0], size if part is None else size // 2, needs,
                       {axis: step(axis, sign)}, views)
                if hop > 1:

                    def add(sign=sign, hop=hop, part=part, ref=ref):
                        into = piece(step(axis, sign * (hop - 1)), part)
                        into[...] = (into[...].astype(F32) + ref[...].astype(F32)).astype(BF16)

                    graph.work(("add", tag, sign, hop - 1), cost, 0,
                               [name] + own_ready(sign * (hop - 1) % n), add)

        def fin():
            finish(piece(mine[axis], None), slot[1, 1], slot[-1, 1])

        graph.work(("fin", tag), 1.5 * cost, 0, [(tag, 1, 1), (tag, -1, 1)] + own_ready(0), fin)

    pool_a, pool_b, pool_m = (slots_a, []), (slots_b, []), (slots_m, [])

    def prepare():
        lane = lax.broadcasted_iota(jnp.int32, (8, BLOCK), 1)
        line = lax.broadcasted_iota(jnp.int32, (8, BLOCK), 0)
        now = jnp.concatenate([seg[...], seg[0:2, :]], axis=0)
        down_one = jnp.concatenate([now[1:8, :], now[0:1, :]], axis=0)
        after = jnp.where(lane == BLOCK - 1, down_one[:, 0:1], pltpu.roll(now, BLOCK - 1, 1))
        keep = jnp.where((line * BLOCK + lane + 1 < counts[0]) & (after == now), 1.0, 0.0).astype(F32)
        marks[...] = jnp.zeros_like(marks)
        marks[pl.ds(0, 8), :] = keep
        columns = marks[...].T
        for copy in local_rows:
            copy.wait()
        for b in range(CAP):
            at = pl.ds(b * BLOCK, BLOCK)
            gradv[at, :] = (gradv[at, :].astype(F32) * columns[:, b : b + 1]).astype(BF16)
        blocks = [pl.ds(b * BLOCK, BLOCK) for b in range(CAP)]
        first_row = pl.multiple_of(x * MSG, 16)
        for t, ref in enumerate((tokv, gradv)):
            for j in range(2):
                xbuf[pl.ds(first_row + (2 * j + t) * BLOCK, BLOCK), :] = blend(leave[j], [ref[at, :] for at in blocks])
        total = jnp.sum(jnp.sum(keep, axis=0, keepdims=True), axis=1, keepdims=True)
        high = jnp.floor(total * (1 / 256))
        middle = jnp.floor((total - 256.0 * high) * (1 / 16))
        low = total - 256.0 * high - 16.0 * middle
        row = lax.broadcasted_iota(jnp.int32, (16, BLOCK), 0) - 3 * x
        digits = jnp.where(row == 0, high, jnp.where(row == 1, middle, jnp.where(row == 2, low, 0.0)))
        xbuf[pl.ds(first_row + 4 * BLOCK, 16), :] = digits.astype(BF16)

    def prepare_own():
        blocks = [pl.ds(b * BLOCK, BLOCK) for b in range(CAP)]
        for t, ref in enumerate((tokv, gradv)):
            for s in range(WORK):
                rows = blend(stay[s][s:], [ref[at, :] for at in blocks[s:]])
                if s < WORK - 1:
                    z[feature, t, pl.ds(s * BLOCK, BLOCK), :] = rows
                else:
                    own3[t] = rows

    graph.work("own", 0.3, 0, [], prepare_own)

    def message(o, part):
        lo, n = (0, MSG) if part is None else ((0, 2 * BLOCK), (2 * BLOCK, MSG - 2 * BLOCK))[part]
        return xbuf.at[pl.ds(pl.multiple_of(o * MSG + lo, 16), n), :]

    mx = spread("mx", "x", MSG * BLOCK * 2, [], lambda o, part, r: message(o, part))

    def select():
        digits = sum(xbuf[pl.ds(i * MSG + 4 * BLOCK, 16), :].astype(F32) for i in range(NX)).astype(BF16)
        for d in range(NY):
            for t in range(2):
                blocks = [xbuf[pl.ds(i // 2 * MSG + (i % 2 * 2 + t) * BLOCK, BLOCK), :] for i in range(2 * NX)]
                ysend[d, pl.ds(t * BLOCK, BLOCK), :] = blend(route[d], blocks)
            ysend[d, pl.ds(2 * BLOCK, 16), :] = digits

    graph.work("select", 0.5, 0, [n for names in mx.values() for n in names], select)
    move_halves = (pl.ds(0, BLOCK), pl.ds(BLOCK, BLOCK + 16))

    def merge(own_ref, one, other):
        total = own_ref[...].astype(F32) + one[...].astype(F32) + other[...].astype(F32)
        for t in range(2):
            z[feature, t, pl.ds(MAIN, BLOCK), :] = (
                total[t * BLOCK : (t + 1) * BLOCK] + own3[t].astype(F32)
            ).astype(BF16)
        own_ref[...] = total.astype(BF16)

    gather_sum("my", "y", YMSG * BLOCK * 2, lambda j: ["select"],
               lambda o, part: ysend.at[o] if part is None else ysend.at[o, move_halves[part], :],
               0.15, merge, pool_m, move_halves)
    merged = ("fin", "my")

    def loss_total():
        digits = ysend[y, pl.ds(2 * BLOCK, 16), :].astype(F32)
        row = lax.broadcasted_iota(jnp.int32, (16, BLOCK), 0) % 3
        parts = jnp.where(row == 0, 256.0 * digits, jnp.where(row == 1, 16.0 * digits, digits))
        return jnp.sum(parts, axis=0, keepdims=True)[:, 0:1]

    row_halves = (pl.ds(0, 32), pl.ds(32, 32))

    def shard(ref, at_y, at_x, cut, part):
        first = pl.multiple_of((at_y * NX + at_x) * ROWS + (32 if part else 0), 32)
        return ref.at[pl.ds(first, ROWS if part is None else 32), pl.ds(*CUT[cut])]

    size_a, size_b = ROWS * CUT["a"][1] * 2, ROWS * CUT["b"][1] * 2
    by = spread("by", "y", size_b, [], lambda o, part, r: shard(w, o, x, "b", part))
    ax = spread("ax", "x", size_a, mx[1] + mx[3], lambda o, part, r: shard(w, y, o, "a", part))
    ay, bx = {}, {}
    for e in ax:
        ay[e] = spread(("ay", e), "y", size_a, ax[e], lambda o, part, r, e=e: shard(w, o, step("x", -e), "a", part))
    for f in by:
        bx[f] = spread(("bx", f), "x", size_b, by[f] or mx[1] + mx[3], lambda o, part, r, f=f: shard(w, step("y", -f), o, "b", part))

    have = {}
    for tag, lo, rows, needs, t in (
        ("zm", 0, MAIN, ["own"], None), ("zl0", MAIN, BLOCK, [merged], 0), ("zl1", MAIN, BLOCK, [merged], 1),
    ):
        def cut(at, part, lo=lo, rows=rows, t=t):
            if t is not None:
                lo, rows = (lo, rows) if part is None else (lo + part * (rows // 2), rows // 2)
                return z.at[at, t, pl.ds(lo, rows), :]
            if part is None:
                return z.at[at, :, pl.ds(lo, rows), :]
            return z.at[at, part, pl.ds(lo, rows), :]

        bytes_all = (2 if t is None else 1) * rows * BLOCK * 2
        arrived = spread(tag, "z", bytes_all, needs, lambda o, part, r, cut=cut: cut(o * 2 + core, part))
        for g, names in arrived.items():
            for i, name in enumerate(names if g else [None]):
                part = i if g == NZ // 2 else None

                def views(receiver, g=g, part=part, cut=cut):
                    ref = cut(step("z", -g) * 2 + (1 - core if receiver else core), part)
                    return ref, ref

                remote(("core", tag, g, i), "core", bytes_all if part is None else bytes_all // 2,
                       [name] if g else needs, {"core": 1 - core}, views)
                have.setdefault(tag[:2], []).append(("core", tag, g, i))
        have[tag[:2]] += [name for names in arrived.values() for name in names]

    seen = []

    def forward(f):
        start = not seen
        seen.append(f)
        at = step("y", -f)
        rows = pl.ds(pl.multiple_of(at * 256, 256), 256)
        slots = pl.ds(0, MAIN)
        for t, lo, hi in ((0, 0, 4), (1, 4, 6)):
            left = jnp.concatenate([z[at * 2, t, slots, :], z[at * 2 + 1, t, slots, :]], axis=1)

            def tile(n, _, left=left):
                cols = pl.ds(pl.multiple_of(n * 256, 256), 256)
                new = jnp.dot(left, w[rows, cols], preferred_element_type=F32)
                acc[slots, cols] = new if start else acc[slots, cols] + new
                return 0

            lax.fori_loop(lo, hi, tile, 0)

    def forward_last():
        slots = pl.ds(MAIN, BLOCK)
        for t, lo, hi in ((0, 0, 2), (1, 2, 3)):
            left = jnp.concatenate([z[c, t, slots, :] for c in range(2 * NZ)], axis=1)

            def tile(n, _, left=left):
                cols = pl.ds(pl.multiple_of(n * 512, 512), 512)
                acc[slots, cols] = jnp.dot(left, w[:, cols], preferred_element_type=F32)
                return 0

            lax.fori_loop(lo, hi, tile, 0)

    all_landed = []
    for f in range(NY):
        landed = [n for e in ay for n in ay[e][f]] + [n for e in bx[f] for n in bx[f][e]]
        all_landed += landed
        graph.work(("fwd", f), 1.3, 2, have["zm"] + landed, lambda f=f: forward(f))
    graph.work("fwd last", 2.5, 2, have["zl"] + all_landed, forward_last)
    parts_of = (("zm", 0, MAIN, 1.1), ("zl", MAIN, BLOCK, 0.5))

    def turn(c, lo, n_rows):
        for t in range(2):
            xt[t, pl.ds(c * BLOCK, BLOCK), pl.ds(lo, n_rows)] = z[c, t, pl.ds(lo, n_rows), :].T

    for tag, lo, n_rows, cost in parts_of:
        for c in range(2 * NZ):
            graph.work(("turn", tag, c), 0.2 * cost, 3, have[tag], lambda c=c, lo=lo, n_rows=n_rows: turn(c, lo, n_rows))

    def pointwise():
        def rows_of(i, _):
            rows = pl.ds(pl.multiple_of(i * 64, 64), 64)
            g, u, b = acc[rows, 0:HID], acc[rows, HID : 2 * HID], acc[rows, 2 * HID : COLS]
            logistic = jax.nn.sigmoid(g)
            activated = g * logistic
            act[rows, 0:HID] = (b * u * logistic * (1.0 + g * (1.0 - logistic))).astype(BF16)
            act[rows, HID : 2 * HID] = (b * activated).astype(BF16)
            act[rows, 2 * HID : COLS] = (activated * u).astype(BF16)
            return 0

        lax.fori_loop(0, 8, rows_of, 0)

    graph.work("pointwise", 0.6, 2, [("fwd", f) for f in range(NY)] + ["fwd last"]
               + [("turn", tag, c) for tag in have for c in range(2 * NZ)], pointwise)

    def store_hidden():
        last = act[pl.ds(MAIN, BLOCK), 2 * HID : COLS]
        for s in range(WORK - 1):
            at = pl.ds(s * BLOCK, BLOCK)
            hidden[at, :] = act[at, 2 * HID : COLS] + last * slot_of[s].astype(BF16)
        stays = 1.0 - (slot_of[0] + slot_of[1] + slot_of[2])
        hidden[pl.ds(MAIN, BLOCK), :] = last * stays.astype(BF16)

    hidden_copy = pltpu.make_async_copy(hidden, hidden_out, own_sem.at[5])
    sums_copy = pltpu.make_async_copy(sums_out, sums_hbm, own_sem.at[6])

    graph.work("hidden", 0.3, 9, [("bwd", 0)], store_hidden)
    graph.work("send hidden", 0.0, 9, [("fin", ("sbx", 0)), "hidden"], hidden_copy.start)

    def backward(j):
        rows = pl.ds(pl.multiple_of(step("y", j) * 256, 256), 256)
        for t, lo, hi in ((0, 0, 2), (1, 2, 3)):
            left = xt[t, rows, :]

            def tile(n, _, left=left):
                cols = pl.ds(pl.multiple_of(n * 512, 512), 512)
                tb[rows, cols] = jnp.dot(left, act[:, cols], preferred_element_type=F32).astype(BF16)
                return 0

            lax.fori_loop(lo, hi, tile, 0)

    for i, j in enumerate((4, 5, 3, 6, 2, 7, 1, 0)):
        graph.work(("bwd", j), 1.0, 1 + i, ["pointwise"], lambda j=j: backward(j))

    def plain(own_ref, one, other):
        own_ref[...] = (own_ref[...].astype(F32) + one[...].astype(F32) + other[...].astype(F32)).astype(BF16)

    def final(cut):
        def run(own_ref, one, other):
            sums = own_ref[...].astype(F32) + one[...].astype(F32) + other[...].astype(F32)
            sums_out[:, pl.ds(*CUT[cut])] = sums / loss_total()
        return run

    for e in (2, 1, 3, 0):
        gather_sum(("say", e), "y", size_a, lambda j: [("bwd", j)],
                   lambda o, part, e=e: shard(tb, o, step("x", e), "a", part), 0.15, plain, pool_a, row_halves)
    for f in (4, 5, 3, 6, 2, 7, 1, 0):
        gather_sum(("sbx", f), "x", size_b, lambda j, f=f: [("bwd", f)],
                   lambda o, part, f=f: shard(tb, step("y", f), o, "b", part), 0.15, plain, pool_b, row_halves)
    gather_sum("sax", "x", size_a, lambda j: [("fin", ("say", j))],
               lambda o, part: shard(tb, y, o, "a", part), 0.15, final("a"), pool_a, row_halves)
    gather_sum("sby", "y", size_b, lambda j: [("fin", ("sbx", j))],
               lambda o, part: shard(tb, o, x, "b", part), 0.15, final("b"), pool_b, row_halves)

    prepare()
    for copy in local:
        copy.wait()
    pl.semaphore_wait(barrier, len(peers))
    copies = {}
    for kind, name in graph.order():
        if kind == "run":
            graph.nodes[name][4]()
        elif kind == "start":
            copies[name] = graph.nodes[name][4](False)
            copies[name].start()
        else:
            graph.nodes[name][4](True).wait_recv()
    sums_copy.start()
    for copy in copies.values():
        copy.wait_send()
    hidden_copy.wait()
    sums_copy.wait()


SENDS = 240


def big(counts, moves, seg, tok, grad, gate, up, down):
    vmem, smem = pl.BlockSpec(memory_space=pltpu.VMEM), pl.BlockSpec(memory_space=pltpu.SMEM)
    anyw = pl.BlockSpec(memory_space=pl.ANY)
    rows = WORK * BLOCK
    return pl.pallas_call(
        big_kernel,
        out_shape=(jax.ShapeDtypeStruct((rows, HID), BF16), jax.ShapeDtypeStruct((ROWS, COLS), F32)),
        in_specs=[smem, smem, vmem] + [anyw] * 5,
        out_specs=(anyw,) * 2,
        scratch_shapes=[
            pltpu.VMEM((NX * NY * ROWS, COLS), BF16),
            pltpu.VMEM((2 * NZ, 2, rows, BLOCK), BF16),
            pltpu.VMEM((2, 2 * NZ * BLOCK, rows), BF16),
            pltpu.VMEM((rows, COLS), F32),
            pltpu.VMEM((rows, COLS), BF16),
            pltpu.VMEM((NX * NY * ROWS, COLS), BF16),
            pltpu.VMEM((36, ROWS, CUT["a"][1]), BF16),
            pltpu.VMEM((40, ROWS, CUT["b"][1]), BF16),
            pltpu.VMEM((8, YMSG, BLOCK), BF16),
            pltpu.VMEM((NX * MSG, BLOCK), BF16),
            pltpu.VMEM((NY, YMSG, BLOCK), BF16),
            pltpu.VMEM((2, BLOCK, BLOCK), BF16),
            pltpu.VMEM((CAP * BLOCK, BLOCK), BF16),
            pltpu.VMEM((CAP * BLOCK, BLOCK), BF16),
            pltpu.VMEM((BLOCK, BLOCK), F32),
            pltpu.VMEM((rows, HID), BF16),
            pltpu.VMEM((ROWS, COLS), F32),
            pltpu.SemaphoreType.DMA((SENDS,)),
            pltpu.SemaphoreType.DMA((SENDS,)),
            pltpu.SemaphoreType.DMA((7,)),
        ],
        compiler_params=pltpu.CompilerParams(
            collective_id=0, has_side_effects=True, vmem_limit_bytes=60 * 1024 * 1024
        ),
    )(counts, moves, seg, tok, grad, gate, up, down)


def finish_kernel(hidden_in, sums, hidden, gate_out, up_out, down_out):
    hidden[...] = hidden_in[...]
    for i, out in enumerate((gate_out, up_out, down_out)):
        out[...] = sums[:, i * HID : (i + 1) * HID]


def finish(hidden, sums):
    vmem = pl.BlockSpec(memory_space=pltpu.VMEM)
    grad = jax.ShapeDtypeStruct((ROWS, HID), F32)
    return pl.pallas_call(
        finish_kernel,
        out_shape=(jax.ShapeDtypeStruct(hidden.shape, BF16), grad, grad, grad),
        in_specs=[vmem, vmem],
        out_specs=(vmem,) * 4,
    )(hidden, sums)


def on_device(tokens, out_grad, counts, block_moves, segment_ids, gate, up, down):
    seg = segment_ids.reshape(CAP, BLOCK)
    hidden, sums = big(counts, block_moves.T, seg, tokens, out_grad, gate, up, down)
    return finish(hidden, sums)


def solution(mesh):
    torus = Mesh(mesh.devices.reshape(NY, NX, NZ, 2), ("y", "x", "z", "core"))
    row, col = ("y", "x"), ("z", "core")
    return jax.shard_map(
        on_device,
        mesh=torus,
        in_specs=(P(row, col), P(row, col), P(row), P(), P(row), P(row, col), P(row, col), P(row, col)),
        out_specs=(P(row, col),) * 4,
        check_vma=False,
    )
```

time: 145 us -> 110 us (0.76)
  Pallas kernels: 133 us -> 108 us
  local copies, waits for them, and re-layouts: 7.17 us -> 0 us
  other arithmetic: 3.12 us -> 0 us
    pallas_call x1, Pallas kernels: 130 us -> 106 us  [big(): pl.pallas_call(big_kernel, out_shape=(jax.ShapeDtypeStruct((rows, HID), B...]
    unnamed x15 -> x0, local copies, waits for them, and re-layouts: 5.83 us -> none
    mul x1 -> x0, other arithmetic: 1.77 us -> none  [on_device(): weighted = out_grad * keep.astype(BF16)[:, None]]
where the time goes in v2:
time: 110 us
  Pallas kernels  108 us (98%)
  between operations  1.29 us (1%)
    pallas_call x1, Pallas kernels, big(): pl.pallas_call(big_kernel, out_shape=(jax.ShapeDtypeStruct((rows, HID), B...  106 us

profile of v2, /device:TPU:1, one launch (start us, length us, event | category | flops | bytes accessed | tf_op | source)
XLA Modules:
  0.0 109.5 jit_solution(2408627407358708224)
XLA Ops:
  1.3 106.1 %shard_map.111 = (bf16[512,512]{1,0:T(8,128)(2,1)}, f32[64,1536]{1,0:T(8,128)}) custom-call(s32[1]{0:T(128)S(6)} %copy.12.counts, s32[3,16]{1,0:T(4,128)} %bitcast.3, s32[6,128]{1,0:T(8,128)} %bitcast.2, bf16[768,128]{1,0:T(8,128)(2,1)} %tok.1, bf16[768,128]{1,0:T(8,128)(2,1)} %grad.1, bf16[64,512]{1,0:T(8,128)(2,1)} %gate.1, bf16[64,512]{1,0:T(8,128)(2,1)} %up.1, ...), custom_call_target="tpu_custom_call" | custom-call | tf_op jit(solution)/shard_map/pallas_call | solution.py:501
  107.4 2.1 %shard_map.112 = (bf16[512,512]{1,0:T(8,128)(2,1)}, f32[64,512]{1,0:T(8,128)}, f32[64,512]{1,0:T(8,128)}, f32[64,512]{1,0:T(8,128)}) custom-call(bf16[512,512]{1,0:T(8,128)(2,1)} %get-tuple-element.6.hidden_in, f32[64,1536]{1,0:T(8,128)} %get-tuple-element.7.sums), custom_call_target="tpu_custom_call" | custom-call | tf_op jit(solution)/shard_map/pallas_call | solution.py:543

commit v3 on v2

v3 whole, which is shorter than its diff:
```python
import jax
import jax.numpy as jnp
from jax import lax
from jax.experimental import pallas as pl
from jax.experimental.pallas import tpu as pltpu
from jax.sharding import Mesh
from jax.sharding import PartitionSpec as P

BLOCK = 128
WORK = 4
CAP = 6
MOVES = 16
NX, NY, NZ = 4, 8, 8
ROWS = 64
HID = 512
PART = HID // 2
COLS = 3 * PART
RANK = WORK * BLOCK
MAIN = 384
MSG = 4 * BLOCK + 16
YMSG = 2 * BLOCK + 16
CUT = {"a": (0, 384), "b": (384, 384)}
LINKS = ("x+", "x-", "y+", "y-", "z+", "z-", "core", "pair")
RING = 6
MESH = pl.DeviceIdType.MESH
BF16, F32 = jnp.bfloat16, jnp.float32


def choose(y, x, pair, counts, moves):
    me = y * NX + x
    count = counts[0]
    zero, one = jnp.int32(0), jnp.int32(1)
    src = [moves[0, m] for m in range(MOVES)]
    dst = [moves[1, m] for m in range(MOVES)]
    blk = [moves[2, m] for m in range(MOVES)]
    src_y = [lax.div(v, jnp.int32(NX)) for v in src]
    src_x = [v - NX * w for v, w in zip(src, src_y)]

    def factor(flag):
        return jnp.where(flag, 1.0, 0.0).astype(F32)

    left = zero
    leaving = [-one] * 2
    arrives = zero
    for m in range(MOVES):
        mine = src[m] == me
        for j in range(2):
            leaving[j] = jnp.where(mine & (left == j), blk[m], leaving[j])
        left = left + jnp.where(mine, one, zero)
        arrives = arrives | jnp.where(dst[m] == me, one, zero)
    kept = zero
    chosen = [-one] * WORK
    for b in range(CAP):
        stays = (b * BLOCK < count) & (leaving[0] != b) & (leaving[1] != b)
        for s in range(WORK):
            chosen[s] = jnp.where(stays & (kept == s), jnp.int32(b), chosen[s])
        kept = kept + jnp.where(stays, one, zero)
    stay = [[factor(chosen[s] == b) for b in range(CAP)] for s in range(WORK)]
    leave = [[factor(leaving[j] == b) for b in range(CAP)] for j in range(2)]

    second = [zero] * MOVES
    for m in range(MOVES):
        for before in range(m):
            second[m] = second[m] | jnp.where(src[before] == src[m], one, zero)
    route = []
    for to_x in (x, pair):
        for d in range(NY):
            at = -one
            for m in range(MOVES):
                hit = (src_y[m] == y) & (dst[m] == d * NX + to_x)
                at = jnp.where(hit, src_x[m] * 2 + second[m], at)
            route.append([factor(at == i) for i in range(2 * NX)])
    slot = [factor((arrives == 1) & (kept == s)) for s in range(WORK)]
    return stay, leave, route, slot


def blend(factors, blocks):
    total = None
    for f, block in zip(factors, blocks):
        term = block * f.astype(BF16)
        total = term if total is None else total + term
    return total


class Graph:
    def __init__(self):
        self.nodes = {}

    def send(self, name, link, size, needs, make, silent):
        self.nodes[name] = ("send", link, size, tuple(needs), make, silent)

    def work(self, name, cost, rank, needs, run):
        self.nodes[name] = ("work", cost, rank, tuple(needs), run)

    rate, lag = 46.6e3, 2.5
    early, late = 0.6, 1.0

    def span(self, n):
        node = self.nodes[n]
        if node[0] == "work":
            return node[1]
        quick = node[1] == "core"
        return node[2] / (self.rate * (12 if quick else 1)) + (1.0 if quick else self.lag)

    def order(self):
        nodes = self.nodes
        after = {n: [] for n in nodes}
        for n, node in nodes.items():
            for m in node[3]:
                after[m].append(n)
        below = {}

        def urgency(n):
            if n not in below:
                below[n] = self.span(n) + max([urgency(m) for m in after[n]], default=0.0)
            return below[n]

        todo = sorted(nodes, key=lambda n: -urgency(n))
        done, flying, free, now, steps, times = set(), [], {}, 0.0, [], {}
        while todo or flying:
            landed = ("fin", ("my", 1)) in done
            for name in [n for n in todo if nodes[n][0] == "send"]:
                _, link, size, needs = nodes[name][:4]
                ways = ("x+", "x-") if link == "pair" else (link,)
                ahead = self.late if landed or link in ("z+", "z-", "core") else self.early
                begin = max([now] + [free.get(way, 0.0) for way in ways])
                if all(n in done for n in needs) and begin - now < ahead:
                    quick = link == "core"
                    ends = begin + size / (self.rate * (12 if quick else 1))
                    for way in ways:
                        free[way] = ends
                    flying.append((ends + (1.0 if quick else self.lag), len(steps), name))
                    steps.append(("start", name))
                    todo.remove(name)
            flying.sort()
            if flying and flying[0][0] <= now:
                name = flying.pop(0)[2]
                if not nodes[name][5]:
                    steps.append(("wait", name))
                times[name] = now
                done.add(name)
                continue
            ready = [n for n in todo if nodes[n][0] == "work" and all(m in done for m in nodes[n][3])]
            if ready:
                steps.append(("run", ready[0]))
                now += nodes[ready[0]][1]
                times[ready[0]] = now
                done.add(ready[0])
                todo.remove(ready[0])
                continue
            if flying:
                now = flying[0][0]
        times["end"] = now
        self.times = times
        return steps


def big_kernel(counts, moves, seg, tok, grad, gate, up, down, hidden_out, sums_hbm,
               w, z, xt, acc, act, tb, tb2, slots_a, slots_o, slots_s, slots_y, slots_m, xbuf, ysend, own3, tokv, gradv,
               marks, hbuf, hidden, sums_out, send_sem, recv_sem, own_sem):
    y, x = lax.axis_index("y"), lax.axis_index("x")
    zz, core = lax.axis_index("z"), lax.axis_index("core")
    size_of = {"x": NX, "y": NY, "z": NZ}
    mine = {"x": x, "y": y, "z": zz}
    side = lax.rem(x, 2)
    pair = x + 1 - 2 * side

    def step(axis, by):
        return lax.rem(mine[axis] + (by % size_of[axis]), size_of[axis])

    barrier = pltpu.get_barrier_semaphore()
    peers = [{axis: step(axis, by)} for axis in ("x", "y", "z") for by in (1, -1)] + [{"core": 1 - core}]
    for peer in peers:
        pl.semaphore_signal(barrier, inc=1, device_id=peer, device_id_type=MESH)

    own_rows = pl.ds(pl.multiple_of((y * NX + x) * ROWS, ROWS), ROWS)
    feature = zz * 2 + core
    local_rows = [
        pltpu.make_async_copy(tok, tokv, own_sem.at[0]),
        pltpu.make_async_copy(grad, gradv, own_sem.at[1]),
    ]
    local = [
        pltpu.make_async_copy(
            ref.at[:, pl.ds(p * PART, PART)], w.at[p, own_rows, pl.ds(i * PART, PART)], own_sem.at[2 + 2 * i + p]
        )
        for i, ref in enumerate((gate, up, down))
        for p in range(2)
    ]
    for copy in local_rows + local:
        copy.start()
    stay, leave, route, slot_of = choose(y, x, pair, counts, moves)

    graph = Graph()
    index = {}

    def remote(name, link, size, needs, peer, views, shared=None):
        i = index.setdefault(shared or name, len(index))

        def make(receiver, at=0):
            source, target = views(receiver)
            return pltpu.make_async_remote_copy(
                src_ref=source, dst_ref=target, send_sem=send_sem.at[at], recv_sem=recv_sem.at[i],
                device_id=peer, device_id_type=MESH,
            )

        graph.send(name, link, size, needs, make, shared is not None)

    def join(shared, members, ref):
        def wait():
            pltpu.make_async_copy(ref(), ref(), recv_sem.at[index[shared]]).wait()

        graph.work(shared, 0.0, 0, members, wait)

    def spread(tag, axis, size, needs, piece):
        n = size_of[axis]
        arrived = {0: list(needs)}
        far = (tag, "far")
        for hop in range(1, n // 2 + 1):
            for sign in (1, -1):
                part = None if hop < n // 2 else (0 if sign > 0 else 1)

                def views(receiver, sign=sign, hop=hop, part=part):
                    ref = piece(step(axis, -sign * (hop if receiver else hop - 1)), part)
                    return ref, ref

                remote((tag, sign, hop), axis + "-+"[sign > 0], size if part is None else size // 2,
                       needs if hop == 1 else [(tag, sign, hop - 1)], {axis: step(axis, sign)}, views,
                       None if part is None else far)
                if part is None:
                    arrived[sign * hop % n] = [(tag, sign, hop)]
        join(far, [(tag, 1, n // 2), (tag, -1, n // 2)], lambda: piece(step(axis, n // 2), None))
        arrived[n // 2] = [far]
        return arrived

    def x_spread(tag, size, needs, other_needs, piece):
        far = (tag, "far")
        for sign in (1, -1):
            part = 0 if sign > 0 else 1
            for hop in (1, 2):
                def same(receiver, sign=sign, hop=hop, part=part):
                    origin = step("x", -sign * (hop if receiver else hop - 1))
                    ref = piece(origin, lax.rem(origin, 2), part)
                    return ref, ref

                remote((tag, sign, hop), "x" + "-+"[sign > 0], size // 2, needs if hop == 1 else [(tag, sign, 1)],
                       {"x": step("x", sign)}, same, None if hop == 1 else far)

            def other(receiver, sign=sign):
                origin = step("x", -sign if receiver else 0)
                ref = piece(origin, 1 - lax.rem(origin, 2), None)
                return ref, ref

            remote((tag, sign, 0), "x" + "-+"[sign > 0], size, other_needs, {"x": step("x", sign)}, other)
        join(far, [(tag, 1, 2), (tag, -1, 2)], lambda: piece(step("x", 2), side, None))
        return {0: list(needs), 1: [(tag, 1, 0)], 3: [(tag, -1, 0)], 2: [far]}

    def gather_sum(tag, axis, size, own_ready, piece, cost, finish, pool, halves):
        n = size_of[axis]
        slot = {}
        slots, used = pool
        for hop in range(n // 2, 0, -1):
            for sign in (1, -1):
                name = (tag, sign, hop)
                part = None if hop < n // 2 else (0 if sign > 0 else 1)
                slot[sign, hop] = ref = slots.at[len(used)]
                used.append(name)
                if part is not None:
                    ref = halves(ref, part)

                def views(receiver, sign=sign, hop=hop, part=part, ref=ref):
                    return piece(step(axis, sign * hop), part), ref

                needs = own_ready(sign * hop % n) if hop == n // 2 else [("add", tag, sign, hop)]
                remote(name, axis + "-+"[sign > 0], size if part is None else size // 2, needs,
                       {axis: step(axis, sign)}, views)
                if hop > 1:

                    def add(sign=sign, hop=hop, part=part, ref=ref):
                        into = piece(step(axis, sign * (hop - 1)), part)
                        into[...] = (into[...].astype(F32) + ref[...].astype(F32)).astype(BF16)

                    graph.work(("add", tag, sign, hop - 1), cost, 0,
                               [name] + own_ready(sign * (hop - 1) % n), add)

        def fin():
            finish(piece(mine[axis], None), slot[1, 1], slot[-1, 1])

        graph.work(("fin", tag), 1.5 * cost, 0, [(tag, 1, 1), (tag, -1, 1)] + own_ready(0), fin)

    def x_sum(tag, size, own_ready, piece, finish, at):
        for sign in (1, -1):
            part = 0 if sign > 0 else 1
            way, peer = "x" + "-+"[sign > 0], {"x": step("x", sign)}
            first, second = slots_s.at[at, 2 * part], slots_s.at[at, 2 * part + 1]
            remote((tag, sign, 2), way, size // 2, own_ready(2), peer,
                   lambda r, part=part, first=first: (piece(step("x", 2), part), first))
            remote((tag, sign, 1), way, size // 2, [(tag, sign, 2)], peer,
                   lambda r, first=first, second=second: (first, second))
            remote((tag, sign, 0), way, size, own_ready(sign % NX), peer,
                   lambda r, sign=sign, part=part: (piece(step("x", sign), None), slots_o.at[at, part]))

        def fin():
            own_ref = piece(x, None)
            own = own_ref[...].astype(F32)
            two_on = jnp.concatenate([slots_s[at, 1], slots_s[at, 3]], axis=0).astype(F32)
            finish(own + two_on, slots_o[at, 0].astype(F32) + slots_o[at, 1].astype(F32))

        graph.work(("fin", tag), 0.15, 0, [(tag, s, h) for s in (1, -1) for h in (1, 0)] + own_ready(0), fin)

    pool_a, pool_y, pool_m = (slots_a, []), (slots_y, []), (slots_m, [])

    def prepare():
        lane = lax.broadcasted_iota(jnp.int32, (8, BLOCK), 1)
        line = lax.broadcasted_iota(jnp.int32, (8, BLOCK), 0)
        now = jnp.concatenate([seg[...], seg[0:2, :]], axis=0)
        down_one = jnp.concatenate([now[1:8, :], now[0:1, :]], axis=0)
        after = jnp.where(lane == BLOCK - 1, down_one[:, 0:1], pltpu.roll(now, BLOCK - 1, 1))
        keep = jnp.where((line * BLOCK + lane + 1 < counts[0]) & (after == now), 1.0, 0.0).astype(F32)
        marks[...] = jnp.zeros_like(marks)
        marks[pl.ds(0, 8), :] = keep
        columns = marks[...].T
        for copy in local_rows:
            copy.wait()
        for b in range(CAP):
            at = pl.ds(b * BLOCK, BLOCK)
            gradv[at, :] = (gradv[at, :].astype(F32) * columns[:, b : b + 1]).astype(BF16)
        blocks = [pl.ds(b * BLOCK, BLOCK) for b in range(CAP)]
        first_row = pl.multiple_of(x * MSG, 16)
        for t, ref in enumerate((tokv, gradv)):
            for j in range(2):
                xbuf[pl.ds(first_row + (2 * j + t) * BLOCK, BLOCK), :] = blend(leave[j], [ref[at, :] for at in blocks])
        total = jnp.sum(jnp.sum(keep, axis=0, keepdims=True), axis=1, keepdims=True)
        high = jnp.floor(total * (1 / 256))
        middle = jnp.floor((total - 256.0 * high) * (1 / 16))
        low = total - 256.0 * high - 16.0 * middle
        row = lax.broadcasted_iota(jnp.int32, (16, BLOCK), 0) - 3 * x
        digits = jnp.where(row == 0, high, jnp.where(row == 1, middle, jnp.where(row == 2, low, 0.0)))
        xbuf[pl.ds(first_row + 4 * BLOCK, 16), :] = digits.astype(BF16)

    def rank_rows(of, lo, n):
        return pl.ds(pl.multiple_of(of * RANK + lo, BLOCK), n)

    def prepare_own():
        blocks = [pl.ds(b * BLOCK, BLOCK) for b in range(CAP)]
        for t, ref in enumerate((tokv, gradv)):
            for s in range(WORK):
                rows = blend(stay[s][s:], [ref[at, :] for at in blocks[s:]])
                if s < WORK - 1:
                    z[feature, t, rank_rows(side, s * BLOCK, BLOCK), :] = rows
                else:
                    own3[0, t] = rows

    graph.work("own", 0.3, 0, [], prepare_own)

    def message(o, part):
        lo, n = (0, MSG) if part is None else ((0, 2 * BLOCK), (2 * BLOCK, MSG - 2 * BLOCK))[part]
        return xbuf.at[pl.ds(pl.multiple_of(o * MSG + lo, 16), n), :]

    mx = spread("mx", "x", MSG * BLOCK * 2, [], message)

    def select(which):
        if which == 0:
            digits = sum(xbuf[pl.ds(i * MSG + 4 * BLOCK, 16), :].astype(F32) for i in range(NX)).astype(BF16)
        else:
            digits = jnp.zeros((16, BLOCK), BF16)
        for d in range(NY):
            for t in range(2):
                blocks = [xbuf[pl.ds(i // 2 * MSG + (i % 2 * 2 + t) * BLOCK, BLOCK), :] for i in range(2 * NX)]
                ysend[which, d, pl.ds(t * BLOCK, BLOCK), :] = blend(route[which * NY + d], blocks)
            ysend[which, d, pl.ds(2 * BLOCK, 16), :] = digits

    move_halves = (pl.ds(0, BLOCK), pl.ds(BLOCK, BLOCK + 16))
    cut_move = lambda ref, part: ref.at[move_halves[part], :]
    remote("own3", "pair", 2 * BLOCK * BLOCK * 2, ["own"] + mx[1] + mx[3], {"x": pair}, lambda r: (own3.at[0], own3.at[1]))
    for which in range(2):
        graph.work(("select", which), 0.6, 0, [n for names in mx.values() for n in names], lambda which=which: select(which))

        def merge(own_ref, one, other, which=which):
            total = own_ref[...].astype(F32) + one[...].astype(F32) + other[...].astype(F32)
            of = side if which == 0 else 1 - side
            for t in range(2):
                z[feature, t, rank_rows(of, MAIN, BLOCK), :] = (
                    total[t * BLOCK : (t + 1) * BLOCK] + own3[which, t].astype(F32)
                ).astype(BF16)
            own_ref[...] = total.astype(BF16)

        ready = [("select", which), "own"] + (["own3"] if which else [])
        gather_sum(("my", which), "y", YMSG * BLOCK * 2,
                   lambda j, which=which, ready=ready: ready if j == 0 else [("select", which)],
                   lambda o, part, which=which: ysend.at[which, o] if part is None else ysend.at[which, o, move_halves[part], :],
                   0.15, merge, pool_m, cut_move)

    def loss_total():
        digits = ysend[0, y, pl.ds(2 * BLOCK, 16), :].astype(F32)
        row = lax.broadcasted_iota(jnp.int32, (16, BLOCK), 0) % 3
        parts = jnp.where(row == 0, 256.0 * digits, jnp.where(row == 1, 16.0 * digits, digits))
        return jnp.sum(parts, axis=0, keepdims=True)[:, 0:1]

    def shard_rows(at_y, at_x, part):
        first = pl.multiple_of((at_y * NX + at_x) * ROWS + (32 if part else 0), 32)
        return pl.ds(first, ROWS if part is None else 32)

    def shard(of, at_y, at_x, cut, part):
        return w.at[of, shard_rows(at_y, at_x, part), pl.ds(*CUT[cut])]

    size_a, size_b = ROWS * CUT["a"][1] * 2, ROWS * CUT["b"][1] * 2
    by_own = spread("by", "y", size_b, [], lambda o, part: shard(side, o, x, "b", part))
    by_other = spread("bz", "y", size_b, [], lambda o, part: shard(1 - side, o, x, "b", part))
    ax = x_spread("ax", size_a, mx[1] + mx[3], mx[1] + mx[3], lambda o, of, part: shard(of, y, o, "a", part))
    ay, bx = {}, {}
    for e in ax:
        ay[e] = spread(("ay", e), "y", size_a, ax[e], lambda o, part, e=e: shard(side, o, step("x", -e), "a", part))
    for f in by_own:
        bx[f] = x_spread(("bx", f), size_b, by_own[f] or mx[1] + mx[3], by_other[f] or mx[1] + mx[3],
                         lambda o, of, part, f=f: shard(of, step("y", -f), o, "b", part))

    def hand(name, lo, n, needs):
        def views(receiver):
            ref = z.at[feature, :, rank_rows(1 - side if receiver else side, lo, n), :]
            return ref, ref

        remote(name, "pair", 2 * n * BLOCK * 2, needs, {"x": pair}, views)

    hand("pm", 0, MAIN, ["own"] + mx[1] + mx[3])
    have, turns = {}, []

    def turn(c, t, of, lo, n_rows):
        rows = rank_rows(of, lo, n_rows)
        xt[t, pl.ds(pl.multiple_of(c * BLOCK, BLOCK), BLOCK), rows] = z[c, t, rows, :].T

    for tag, of, lo, rows, needs in (
        ("zm", side, 0, MAIN, ["own"]), ("zp", 1 - side, 0, MAIN, ["pm"]),
        ("zl", side, MAIN, BLOCK, [("fin", ("my", 0))]), ("zq", 1 - side, MAIN, BLOCK, [("fin", ("my", 1))]),
    ):
        have[tag] = []
        for t in range(2):
            def cut(at, part, of=of, lo=lo, rows=rows, t=t):
                if part is None:
                    return z.at[at, t, rank_rows(of, lo, rows), :]
                first = pl.multiple_of(of * RANK + lo + part * (rows // 2), 64)
                return z.at[at, t, pl.ds(first, rows // 2), :]

            size = rows * BLOCK * 2
            arrived = spread((tag, t), "z", size, needs, lambda o, part, cut=cut: cut(o * 2 + core, part))
            shared = ("core", tag, t)
            for g, names in arrived.items():
                def views(receiver, g=g, cut=cut):
                    ref = cut(step("z", -g) * 2 + (1 - core if receiver else core), None)
                    return ref, ref

                remote((shared, g), "core", size, names, {"core": 1 - core}, views, shared)
            join(shared, [(shared, g) for g in arrived],
                 lambda of=of, lo=lo, rows=rows, t=t: z.at[pl.ds(0, NZ), t, rank_rows(of, lo, rows), :])
            have[tag] += [shared] + [name for names in arrived.values() for name in names]
            for g, names in arrived.items():
                for far in range(2):
                    turns.append(("turn", tag, t, g, far))
                    graph.work(turns[-1], 0.1 if lo == 0 else 0.04, 3, [shared] if far else names,
                               lambda g=g, far=far, t=t, of=of, lo=lo, rows=rows: turn(
                                   step("z", -g) * 2 + (1 - core if far else core), t, of, lo, rows))
    last_needs = have["zl"] + have["zq"]

    seen = []

    def forward(f, tag, of):
        start = tag not in seen
        seen.append(tag)
        at = step("y", -f)
        rows = pl.ds(pl.multiple_of(at * 256, 256), 256)
        slots = rank_rows(of, 0, MAIN)
        for t, lo, n in ((0, 0, 2 * PART), (1, 2 * PART, PART)):
            left = jnp.concatenate([z[at * 2, t, slots, :], z[at * 2 + 1, t, slots, :]], axis=1)
            cols = pl.ds(lo, n)
            new = jnp.dot(left, w[side, rows, cols], preferred_element_type=F32)
            acc[slots, cols] = new if start else acc[slots, cols] + new

    last_rows = [pl.ds(p * RANK + MAIN, BLOCK) for p in range(2)]

    def forward_last():
        for t, lo, hi in ((0, 0, 2), (1, 2, 3)):
            left = jnp.concatenate(
                [jnp.concatenate([z[c, t, slots, :] for c in range(2 * NZ)], axis=1) for slots in last_rows], axis=0
            )

            def tile(n, _, left=left):
                cols = pl.ds(pl.multiple_of(n * PART, PART), PART)
                new = jnp.dot(left, w[side, :, cols], preferred_element_type=F32)
                for p, slots in enumerate(last_rows):
                    acc[slots, cols] = new[p * BLOCK : (p + 1) * BLOCK]
                return 0

            lax.fori_loop(lo, hi, tile, 0)

    all_landed = []
    for f in range(NY):
        landed = [n for e in ay for n in ay[e][f]] + [n for e in bx[f] for n in bx[f][e]]
        all_landed += landed
        for tag, of in (("zm", side), ("zp", 1 - side)):
            graph.work(("fwd", tag, f), 0.6, 2, have[tag] + landed, lambda f=f, tag=tag, of=of: forward(f, tag, of))
    graph.work("fwd last", 1.3, 2, last_needs + all_landed, forward_last)

    def pointwise():
        def rows_of(i, _):
            rows = pl.ds(pl.multiple_of(i * 64, 64), 64)
            g, u, b = acc[rows, 0:PART], acc[rows, PART : 2 * PART], acc[rows, 2 * PART : COLS]
            logistic = jax.nn.sigmoid(g)
            activated = g * logistic
            act[rows, 0:PART] = (b * u * logistic * (1.0 + g * (1.0 - logistic))).astype(BF16)
            act[rows, PART : 2 * PART] = (b * activated).astype(BF16)
            act[rows, 2 * PART : COLS] = (activated * u).astype(BF16)
            return 0

        lax.fori_loop(0, 16, rows_of, 0)

    graph.work("pointwise", 0.6, 2, [("fwd", tag, f) for tag in ("zm", "zp") for f in range(NY)] + ["fwd last"] + turns, pointwise)

    for i in range(WORK):
        def views(receiver, i=i):
            here = act.at[rank_rows(1 - side, i * BLOCK, BLOCK), pl.ds(2 * PART, PART)]
            return here, hbuf.at[pl.ds(i * BLOCK, BLOCK), :]

        remote(("hidden", i), "pair", BLOCK * PART * 2, [("bwd", 0)] if i else ["pointwise"], {"x": pair}, views)

    def store_hidden():
        stays = 1.0 - (slot_of[0] + slot_of[1] + slot_of[2])
        for which in range(2):
            cols = pl.ds(pl.multiple_of((side if which == 0 else 1 - side) * PART, PART), PART)

            def rows(s, which=which):
                if which == 0:
                    return act[rank_rows(side, s * BLOCK, BLOCK), 2 * PART : COLS]
                return hbuf[pl.ds(s * BLOCK, BLOCK), :]

            last = rows(WORK - 1)
            for s in range(WORK - 1):
                hidden[pl.ds(s * BLOCK, BLOCK), cols] = rows(s) + last * slot_of[s].astype(BF16)
            hidden[pl.ds(MAIN, BLOCK), cols] = last * stays.astype(BF16)

    hidden_copy = pltpu.make_async_copy(hidden, hidden_out, own_sem.at[8])
    sums_copy = pltpu.make_async_copy(sums_out, sums_hbm, own_sem.at[9])
    graph.work("store hidden", 0.3, 9, [("hidden", i) for i in range(WORK)], store_hidden)
    graph.work("send hidden", 0.0, 9, ["store hidden"], hidden_copy.start)

    def backward(j):
        rows = pl.ds(pl.multiple_of(step("y", j) * 256, 256), 256)
        for t, lo, n in ((0, 0, 2 * PART), (1, 2 * PART, PART)):
            cols = pl.ds(lo, n)
            tb[rows, cols] = jnp.dot(xt[t, rows, :], act[:, cols], preferred_element_type=F32).astype(BF16)

    for i, j in enumerate((4, 5, 3, 6, 2, 7, 1, 0)):
        graph.work(("bwd", j), 0.9, 1 + i, ["pointwise"], lambda j=j: backward(j))

    def plain(own_ref, one, other):
        own_ref[...] = (own_ref[...].astype(F32) + one[...].astype(F32) + other[...].astype(F32)).astype(BF16)

    def final_a(same, other):
        total = loss_total()
        sums_out[side, :, pl.ds(*CUT["a"])] = same / total
        sums_out[1 - side, :, pl.ds(*CUT["a"])] = other / total

    def final_b(p):
        def run(own_ref, one, other):
            sums = own_ref[...].astype(F32) + one[...].astype(F32) + other[...].astype(F32)
            sums_out[p, :, pl.ds(*CUT["b"])] = sums / loss_total()
        return run

    def term(at_y, at_x, cut, part):
        return tb.at[shard_rows(at_y, at_x, part), pl.ds(*CUT[cut])]

    row_halves = (pl.ds(0, 32), pl.ds(32, 32))
    for e in (2, 1, 3, 0):
        gather_sum(("say", e), "y", size_a, lambda j: [("bwd", j)],
                   lambda o, part, e=e: term(o, step("x", e), "a", part), 0.1, plain, pool_a,
                   lambda ref, part: ref.at[row_halves[part], :])
    for f in (4, 5, 3, 6, 2, 7, 1, 0):
        def keep(same, other, f=f):
            at = step("y", f)
            tb2[at, side] = same.astype(BF16)
            tb2[at, 1 - side] = other.astype(BF16)

        x_sum(("sbx", f), size_b, lambda e, f=f: [("bwd", f)],
              lambda o, part, f=f: term(step("y", f), o, "b", part), keep, f)
    x_sum("sax", size_a, lambda e: [("fin", ("say", e))], lambda o, part: term(y, o, "a", part), final_a, NY)

    for p in range(2):
        gather_sum(("sby", p), "y", size_b, lambda j: [("fin", ("sbx", j))],
                   lambda o, part, p=p: tb2.at[o, p] if part is None else tb2.at[o, p, row_halves[part], :], 0.1,
                   final_b(p), pool_y, lambda ref, part: ref.at[row_halves[part], :])

    prepare()
    for copy in local:
        copy.wait()
    pl.semaphore_wait(barrier, len(peers))
    started = {link: [] for link in LINKS}
    for kind, name in graph.order():
        node = graph.nodes[name]
        if kind == "run":
            node[4]()
        elif kind == "start":
            mates = started[node[1]]
            if len(mates) >= RING:
                mates[-RING].wait_send()
            copy = node[4](False, LINKS.index(node[1]) * RING + len(mates) % RING)
            copy.start()
            mates.append(copy)
        else:
            node[4](True).wait_recv()
    sums_copy.start()
    for mates in started.values():
        for copy in mates[-RING:]:
            copy.wait_send()
    hidden_copy.wait()
    sums_copy.wait()
    assert len(index) == RECEIVES


RECEIVES = 278


def big(counts, moves, seg, tok, grad, gate, up, down):
    vmem, smem = pl.BlockSpec(memory_space=pltpu.VMEM), pl.BlockSpec(memory_space=pltpu.SMEM)
    anyw = pl.BlockSpec(memory_space=pl.ANY)
    width = NX * NY * ROWS
    wide_a, wide_b = CUT["a"][1], CUT["b"][1]
    return pl.pallas_call(
        big_kernel,
        out_shape=(jax.ShapeDtypeStruct((RANK, HID), BF16), jax.ShapeDtypeStruct((2, ROWS, COLS), F32)),
        in_specs=[smem, smem, vmem] + [anyw] * 5,
        out_specs=(anyw,) * 2,
        scratch_shapes=[
            pltpu.VMEM((2, width, COLS), BF16),
            pltpu.VMEM((2 * NZ, 2, 2 * RANK, BLOCK), BF16),
            pltpu.VMEM((2, width, 2 * RANK), BF16),
            pltpu.VMEM((2 * RANK, COLS), F32),
            pltpu.VMEM((2 * RANK, COLS), BF16),
            pltpu.VMEM((width, COLS), BF16),
            pltpu.VMEM((NY, 2, ROWS, wide_b), BF16),
            pltpu.VMEM((32, ROWS, wide_a), BF16),
            pltpu.VMEM((NY + 1, 2, ROWS, wide_b), BF16),
            pltpu.VMEM((NY + 1, 4, ROWS // 2, wide_b), BF16),
            pltpu.VMEM((16, ROWS, wide_b), BF16),
            pltpu.VMEM((16, YMSG, BLOCK), BF16),
            pltpu.VMEM((NX * MSG, BLOCK), BF16),
            pltpu.VMEM((2, NY, YMSG, BLOCK), BF16),
            pltpu.VMEM((2, 2, BLOCK, BLOCK), BF16),
            pltpu.VMEM((CAP * BLOCK, BLOCK), BF16),
            pltpu.VMEM((CAP * BLOCK, BLOCK), BF16),
            pltpu.VMEM((BLOCK, BLOCK), F32),
            pltpu.VMEM((RANK, PART), BF16),
            pltpu.VMEM((RANK, HID), BF16),
            pltpu.VMEM((2, ROWS, COLS), F32),
            pltpu.SemaphoreType.DMA((RING * len(LINKS),)),
            pltpu.SemaphoreType.DMA((RECEIVES,)),
            pltpu.SemaphoreType.DMA((10,)),
        ],
        compiler_params=pltpu.CompilerParams(
            collective_id=0, has_side_effects=True, vmem_limit_bytes=60 * 1024 * 1024
        ),
    )(counts, moves, seg, tok, grad, gate, up, down)


def finish_kernel(hidden_in, sums, hidden, gate_out, up_out, down_out, rows, grads, sems):
    quarter = RANK // 4
    ins = [
        pltpu.make_async_copy(hidden_in.at[pl.ds(i * quarter, quarter), :], rows.at[pl.ds(i * quarter, quarter), :], sems.at[i])
        for i in range(4)
    ]
    ins += [
        pltpu.make_async_copy(
            sums.at[p, :, pl.ds(i * PART, PART)], grads.at[i, :, pl.ds(p * PART, PART)], sems.at[4 + 2 * i + p]
        )
        for i in range(3)
        for p in range(2)
    ]
    outs = [
        pltpu.make_async_copy(rows.at[pl.ds(i * quarter, quarter), :], hidden.at[pl.ds(i * quarter, quarter), :], sems.at[10 + i])
        for i in range(4)
    ]
    outs += [pltpu.make_async_copy(grads.at[i], ref, sems.at[14 + i]) for i, ref in enumerate((gate_out, up_out, down_out))]
    for copy in ins:
        copy.start()
    for i in range(4):
        ins[i].wait()
        outs[i].start()
    for i in range(3):
        ins[4 + 2 * i].wait()
        ins[5 + 2 * i].wait()
        outs[4 + i].start()
    for copy in outs:
        copy.wait()


def finish(hidden, sums):
    anyw = pl.BlockSpec(memory_space=pl.ANY)
    grad = jax.ShapeDtypeStruct((ROWS, HID), F32)
    return pl.pallas_call(
        finish_kernel,
        out_shape=(jax.ShapeDtypeStruct(hidden.shape, BF16), grad, grad, grad),
        in_specs=[anyw] * 2,
        out_specs=(anyw,) * 4,
        scratch_shapes=[
            pltpu.VMEM(hidden.shape, BF16),
            pltpu.VMEM((3, ROWS, HID), F32),
            pltpu.SemaphoreType.DMA((17,)),
        ],
    )(hidden, sums)


def on_device(tokens, out_grad, counts, block_moves, segment_ids, gate, up, down):
    seg = segment_ids.reshape(CAP, BLOCK)
    hidden, sums = big(counts, block_moves.T, seg, tokens, out_grad, gate, up, down)
    return finish(hidden, sums)


def solution(mesh):
    torus = Mesh(mesh.devices.reshape(NY, NX, NZ, 2), ("y", "x", "z", "core"))
    row, col = ("y", "x"), ("z", "core")
    return jax.shard_map(
        on_device,
        mesh=torus,
        in_specs=(P(row, col), P(row, col), P(row), P(), P(row), P(row, col), P(row, col), P(row, col)),
        out_specs=(P(row, col),) * 4,
        check_vma=False,
    )
```

time: 110 us -> 98.9 us (0.90)
  Pallas kernels: 108 us -> 97.3 us
    pallas_call x1, Pallas kernels: 106 us -> 95.2 us  [big(): pl.pallas_call(big_kernel, out_shape=(jax.ShapeDtypeStruct((RANK, HID), B...]
where the time goes in v3:
time: 98.9 us; the launch traced here: 98.7 us
  Pallas kernels  97.3 us (98%)
  between operations  1.45 us (1%)
    pallas_call x1, Pallas kernels, big(): pl.pallas_call(big_kernel, out_shape=(jax.ShapeDtypeStruct((RANK, HID), B...  95.2 us
    pallas_call x1, Pallas kernels, finish(): pl.pallas_call(finish_kernel, out_shape=(jax.ShapeDtypeStruct(hidden.shap...  2.03 us

profile of v3, /device:TPU:1, one launch (start us, length us, event | category | flops | bytes accessed | tf_op | source)
XLA Modules:
  0.0 98.7 jit_solution(1166807745618829840)
XLA Ops:
  1.3 95.2 %shard_map.111 = (bf16[512,512]{1,0:T(8,128)(2,1)}, f32[2,64,768]{2,1,0:T(8,128)}) custom-call(s32[1]{0:T(128)S(6)} %copy.12.counts, s32[3,16]{1,0:T(4,128)} %bitcast.3, s32[6,128]{1,0:T(8,128)} %bitcast.2, bf16[768,128]{1,0:T(8,128)(2,1)} %tok.1, bf16[768,128]{1,0:T(8,128)(2,1)} %grad.1, bf16[64,512]{1,0:T(8,128)(2,1)} %gate.1, bf16[64,512]{1,0:T(8,128)(2,1)} %up.1, ...), custom_call_target="tpu_custom_call" | custom-call | tf_op jit(solution)/shard_map/pallas_call | solution.py:625
  96.5 2.0 %shard_map.112 = (bf16[512,512]{1,0:T(8,128)(2,1)}, f32[64,512]{1,0:T(8,128)}, f32[64,512]{1,0:T(8,128)}, f32[64,512]{1,0:T(8,128)}) custom-call(bf16[512,512]{1,0:T(8,128)(2,1)} %get-tuple-element.6.hidden_in, f32[2,64,768]{2,1,0:T(8,128)} %get-tuple-element.7.sums), custom_call_target="tpu_custom_call" | custom-call | tf_op jit(solution)/shard_map/pallas_call | solution.py:696

commit v4 on v3

--- a/solution.py
+++ b/solution.py
@@ -1,3 +1,5 @@
+import random
+
 import jax
 import jax.numpy as jnp
 from jax import lax
@@ -17,37 +19,30 @@
 COLS = 3 * PART
 RANK = WORK * BLOCK
 MAIN = 384
-MSG = 4 * BLOCK + 16
-YMSG = 2 * BLOCK + 16
+MSG = 2 * BLOCK + 16
+YMSG = BLOCK + 16
 CUT = {"a": (0, 384), "b": (384, 384)}
 LINKS = ("x+", "x-", "y+", "y-", "z+", "z-", "core", "pair")
-RING = 6
+RING = 4
 MESH = pl.DeviceIdType.MESH
 BF16, F32 = jnp.bfloat16, jnp.float32
 
 
-def choose(y, x, pair, counts, moves):
-    me = y * NX + x
-    count = counts[0]
+def factor(flag):
+    return jnp.where(flag, 1.0, 0.0).astype(F32)
+
+
+def choose(me, count, moves):
     zero, one = jnp.int32(0), jnp.int32(1)
-    src = [moves[0, m] for m in range(MOVES)]
-    dst = [moves[1, m] for m in range(MOVES)]
-    blk = [moves[2, m] for m in range(MOVES)]
-    src_y = [lax.div(v, jnp.int32(NX)) for v in src]
-    src_x = [v - NX * w for v, w in zip(src, src_y)]
-
-    def factor(flag):
-        return jnp.where(flag, 1.0, 0.0).astype(F32)
-
     left = zero
     leaving = [-one] * 2
     arrives = zero
     for m in range(MOVES):
-        mine = src[m] == me
+        mine = moves[0, m] == me
         for j in range(2):
-            leaving[j] = jnp.where(mine & (left == j), blk[m], leaving[j])
+            leaving[j] = jnp.where(mine & (left == j), moves[2, m], leaving[j])
         left = left + jnp.where(mine, one, zero)
-        arrives = arrives | jnp.where(dst[m] == me, one, zero)
+        arrives = arrives | jnp.where(moves[1, m] == me, one, zero)
     kept = zero
     chosen = [-one] * WORK
     for b in range(CAP):
@@ -57,21 +52,29 @@
         kept = kept + jnp.where(stays, one, zero)
     stay = [[factor(chosen[s] == b) for b in range(CAP)] for s in range(WORK)]
     leave = [[factor(leaving[j] == b) for b in range(CAP)] for j in range(2)]
-
-    second = [zero] * MOVES
+    slot = [factor((arrives == 1) & (kept == s)) for s in range(WORK)]
+    return stay, leave, slot
+
+
+def routes(y, columns, moves):
+    zero, one = jnp.int32(0), jnp.int32(1)
+    src = [moves[0, m] for m in range(MOVES)]
+    dst = [moves[1, m] for m in range(MOVES)]
+    number = []
     for m in range(MOVES):
+        second = zero
         for before in range(m):
-            second[m] = second[m] | jnp.where(src[before] == src[m], one, zero)
-    route = []
-    for to_x in (x, pair):
+            second = second | jnp.where(src[before] == src[m], one, zero)
+        here = (src[m] >= y * NX) & (src[m] < y * NX + NX)
+        number.append(jnp.where(here, (src[m] - y * NX) * 2 + second, -one))
+    result = []
+    for to_x in columns:
         for d in range(NY):
             at = -one
             for m in range(MOVES):
-                hit = (src_y[m] == y) & (dst[m] == d * NX + to_x)
-                at = jnp.where(hit, src_x[m] * 2 + second[m], at)
-            route.append([factor(at == i) for i in range(2 * NX)])
-    slot = [factor((arrives == 1) & (kept == s)) for s in range(WORK)]
-    return stay, leave, route, slot
+                at = jnp.where(dst[m] == d * NX + to_x, number[m], at)
+            result.append([factor(at == i) for i in range(2 * NX)])
+    return result
 
 
 def blend(factors, blocks):
@@ -93,7 +96,8 @@
         self.nodes[name] = ("work", cost, rank, tuple(needs), run)
 
     rate, lag = 46.6e3, 2.5
-    early, late = 0.6, 1.0
+    early, late, along_z = 0.6, 1.0, 1.0
+    seed, noise = 0, 0.0
 
     def span(self, n):
         node = self.nodes[n]
@@ -115,14 +119,16 @@
                 below[n] = self.span(n) + max([urgency(m) for m in after[n]], default=0.0)
             return below[n]
 
-        todo = sorted(nodes, key=lambda n: -urgency(n))
+        draw = random.Random(self.seed)
+        moved = {n: urgency(n) + draw.uniform(0.0, self.noise) for n in nodes}
+        todo = sorted(nodes, key=lambda n: -moved[n])
         done, flying, free, now, steps, times = set(), [], {}, 0.0, [], {}
         while todo or flying:
-            landed = ("fin", ("my", 1)) in done
+            landed = ("fin", ("my", 1, 1)) in done
             for name in [n for n in todo if nodes[n][0] == "send"]:
                 _, link, size, needs = nodes[name][:4]
                 ways = ("x+", "x-") if link == "pair" else (link,)
-                ahead = self.late if landed or link in ("z+", "z-", "core") else self.early
+                ahead = self.along_z if link in ("z+", "z-", "core") else self.late if landed else self.early
                 begin = max([now] + [free.get(way, 0.0) for way in ways])
                 if all(n in done for n in needs) and begin - now < ahead:
                     quick = link == "core"
@@ -155,9 +161,9 @@
         return steps
 
 
-def big_kernel(counts, moves, seg, tok, grad, gate, up, down, hidden_out, sums_hbm,
+def big_kernel(counts_hbm, moves_hbm, seg_hbm, tok, grad, gate, up, down, hidden, sums_out,
                w, z, xt, acc, act, tb, tb2, slots_a, slots_o, slots_s, slots_y, slots_m, xbuf, ysend, own3, tokv, gradv,
-               marks, hbuf, hidden, sums_out, send_sem, recv_sem, own_sem):
+               marks, hbuf, counts, moves, seg, send_sem, recv_sem, own_sem):
     y, x = lax.axis_index("y"), lax.axis_index("x")
     zz, core = lax.axis_index("z"), lax.axis_index("core")
     size_of = {"x": NX, "y": NY, "z": NZ}
@@ -186,9 +192,16 @@
         for i, ref in enumerate((gate, up, down))
         for p in range(2)
     ]
-    for copy in local_rows + local:
+    small = [
+        pltpu.make_async_copy(ref, held, own_sem.at[8 + i])
+        for i, (ref, held) in enumerate(((counts_hbm, counts), (moves_hbm, moves), (seg_hbm, seg)))
+    ]
+    for copy in small + local_rows + local:
         copy.start()
-    stay, leave, route, slot_of = choose(y, x, pair, counts, moves)
+    for copy in small:
+        copy.wait()
+    stay, leave, slot_of = choose(y * NX + x, counts[0], moves)
+    route = []
 
     graph = Graph()
     index = {}
@@ -211,11 +224,11 @@
 
         graph.work(shared, 0.0, 0, members, wait)
 
-    def spread(tag, axis, size, needs, piece):
+    def spread(tag, axis, size, needs, piece, to_far=True):
         n = size_of[axis]
         arrived = {0: list(needs)}
         far = (tag, "far")
-        for hop in range(1, n // 2 + 1):
+        for hop in range(1, n // 2 + to_far):
             for sign in (1, -1):
                 part = None if hop < n // 2 else (0 if sign > 0 else 1)
 
@@ -228,11 +241,12 @@
                        None if part is None else far)
                 if part is None:
                     arrived[sign * hop % n] = [(tag, sign, hop)]
-        join(far, [(tag, 1, n // 2), (tag, -1, n // 2)], lambda: piece(step(axis, n // 2), None))
-        arrived[n // 2] = [far]
+        if to_far:
+            join(far, [(tag, 1, n // 2), (tag, -1, n // 2)], lambda: piece(step(axis, n // 2), None))
+            arrived[n // 2] = [far]
         return arrived
 
-    def x_spread(tag, size, needs, other_needs, piece):
+    def x_spread(tag, size, needs, other_needs, piece, forwarded):
         far = (tag, "far")
         for sign in (1, -1):
             part = 0 if sign > 0 else 1
@@ -250,14 +264,19 @@
                 ref = piece(origin, 1 - lax.rem(origin, 2), None)
                 return ref, ref
 
-            remote((tag, sign, 0), "x" + "-+"[sign > 0], size, other_needs, {"x": step("x", sign)}, other)
-        join(far, [(tag, 1, 2), (tag, -1, 2)], lambda: piece(step("x", 2), side, None))
-        return {0: list(needs), 1: [(tag, 1, 0)], 3: [(tag, -1, 0)], 2: [far]}
+            remote((tag, sign, 0), "x" + "-+"[sign > 0], size, other_needs, {"x": step("x", sign)}, other,
+                   None if forwarded else far)
+        if forwarded:
+            join(far, [(tag, 1, 2), (tag, -1, 2)], lambda: slots_a.at[0])
+            return {0: list(needs), 1: [(tag, 1, 0)], 3: [(tag, -1, 0)], 2: [far]}
+        join(far, [(tag, sign, hop) for sign in (1, -1) for hop in (0, 2)], lambda: slots_a.at[pl.ds(0, 3)])
+        return {0: list(needs), 1: [far], 3: [far], 2: [far]}
 
     def gather_sum(tag, axis, size, own_ready, piece, cost, finish, pool, halves):
         n = size_of[axis]
         slot = {}
         slots, used = pool
+        near = (tag, "near")
         for hop in range(n // 2, 0, -1):
             for sign in (1, -1):
                 name = (tag, sign, hop)
@@ -272,7 +291,7 @@
 
                 needs = own_ready(sign * hop % n) if hop == n // 2 else [("add", tag, sign, hop)]
                 remote(name, axis + "-+"[sign > 0], size if part is None else size // 2, needs,
-                       {axis: step(axis, sign)}, views)
+                       {axis: step(axis, sign)}, views, None if hop > 1 else near)
                 if hop > 1:
 
                     def add(sign=sign, hop=hop, part=part, ref=ref):
@@ -285,9 +304,11 @@
         def fin():
             finish(piece(mine[axis], None), slot[1, 1], slot[-1, 1])
 
-        graph.work(("fin", tag), 1.5 * cost, 0, [(tag, 1, 1), (tag, -1, 1)] + own_ready(0), fin)
+        join(near, [(tag, 1, 1), (tag, -1, 1)], lambda: slots.at[pl.ds(0, 2)])
+        graph.work(("fin", tag), 1.5 * cost, 0, [near] + own_ready(0), fin)
 
     def x_sum(tag, size, own_ready, piece, finish, at):
+        near = (tag, "near")
         for sign in (1, -1):
             part = 0 if sign > 0 else 1
             way, peer = "x" + "-+"[sign > 0], {"x": step("x", sign)}
@@ -295,9 +316,9 @@
             remote((tag, sign, 2), way, size // 2, own_ready(2), peer,
                    lambda r, part=part, first=first: (piece(step("x", 2), part), first))
             remote((tag, sign, 1), way, size // 2, [(tag, sign, 2)], peer,
-                   lambda r, first=first, second=second: (first, second))
+                   lambda r, first=first, second=second: (first, second), near)
             remote((tag, sign, 0), way, size, own_ready(sign % NX), peer,
-                   lambda r, sign=sign, part=part: (piece(step("x", sign), None), slots_o.at[at, part]))
+                   lambda r, sign=sign, part=part: (piece(step("x", sign), None), slots_o.at[at, part]), near)
 
         def fin():
             own_ref = piece(x, None)
@@ -305,7 +326,8 @@
             two_on = jnp.concatenate([slots_s[at, 1], slots_s[at, 3]], axis=0).astype(F32)
             finish(own + two_on, slots_o[at, 0].astype(F32) + slots_o[at, 1].astype(F32))
 
-        graph.work(("fin", tag), 0.15, 0, [(tag, s, h) for s in (1, -1) for h in (1, 0)] + own_ready(0), fin)
+        join(near, [(tag, s, h) for s in (1, -1) for h in (1, 0)], lambda: slots_a.at[pl.ds(0, 3)])
+        graph.work(("fin", tag), 0.15, 0, [near] + own_ready(0), fin)
 
     pool_a, pool_y, pool_m = (slots_a, []), (slots_y, []), (slots_m, [])
 
@@ -325,17 +347,17 @@
             at = pl.ds(b * BLOCK, BLOCK)
             gradv[at, :] = (gradv[at, :].astype(F32) * columns[:, b : b + 1]).astype(BF16)
         blocks = [pl.ds(b * BLOCK, BLOCK) for b in range(CAP)]
-        first_row = pl.multiple_of(x * MSG, 16)
         for t, ref in enumerate((tokv, gradv)):
             for j in range(2):
-                xbuf[pl.ds(first_row + (2 * j + t) * BLOCK, BLOCK), :] = blend(leave[j], [ref[at, :] for at in blocks])
+                xbuf[t, x, pl.ds(j * BLOCK, BLOCK), :] = blend(leave[j], [ref[at, :] for at in blocks])
         total = jnp.sum(jnp.sum(keep, axis=0, keepdims=True), axis=1, keepdims=True)
         high = jnp.floor(total * (1 / 256))
         middle = jnp.floor((total - 256.0 * high) * (1 / 16))
         low = total - 256.0 * high - 16.0 * middle
         row = lax.broadcasted_iota(jnp.int32, (16, BLOCK), 0) - 3 * x
         digits = jnp.where(row == 0, high, jnp.where(row == 1, middle, jnp.where(row == 2, low, 0.0)))
-        xbuf[pl.ds(first_row + 4 * BLOCK, 16), :] = digits.astype(BF16)
+        for t in range(2):
+            xbuf[t, x, pl.ds(2 * BLOCK, 16), :] = digits.astype(BF16)
 
     def rank_rows(of, lo, n):
         return pl.ds(pl.multiple_of(of * RANK + lo, BLOCK), n)
@@ -352,46 +374,47 @@
 
     graph.work("own", 0.3, 0, [], prepare_own)
 
-    def message(o, part):
-        lo, n = (0, MSG) if part is None else ((0, 2 * BLOCK), (2 * BLOCK, MSG - 2 * BLOCK))[part]
-        return xbuf.at[pl.ds(pl.multiple_of(o * MSG + lo, 16), n), :]
-
-    mx = spread("mx", "x", MSG * BLOCK * 2, [], message)
-
-    def select(which):
-        if which == 0:
-            digits = sum(xbuf[pl.ds(i * MSG + 4 * BLOCK, 16), :].astype(F32) for i in range(NX)).astype(BF16)
-        else:
-            digits = jnp.zeros((16, BLOCK), BF16)
+    graph.work("route", 0.5, 0, [], lambda: route.extend(routes(y, (x, pair), moves)))
+    mx = []
+    for t in range(2):
+        def message(o, part, t=t):
+            lo, n = (0, MSG) if part is None else ((0, BLOCK), (BLOCK, MSG - BLOCK))[part]
+            return xbuf.at[t, o, pl.ds(lo, n), :]
+
+        mx.append(spread(("mx", t), "x", MSG * BLOCK * 2, [], message))
+    mx_first = mx[0][1] + mx[0][3] + mx[1][1] + mx[1][3]
+
+    def select(which, t):
+        digits = sum(xbuf[t, i, pl.ds(2 * BLOCK, 16), :].astype(F32) for i in range(NX)).astype(BF16)
+        blocks = [xbuf[t, i // 2, pl.ds(i % 2 * BLOCK, BLOCK), :] for i in range(2 * NX)]
         for d in range(NY):
-            for t in range(2):
-                blocks = [xbuf[pl.ds(i // 2 * MSG + (i % 2 * 2 + t) * BLOCK, BLOCK), :] for i in range(2 * NX)]
-                ysend[which, d, pl.ds(t * BLOCK, BLOCK), :] = blend(route[which * NY + d], blocks)
-            ysend[which, d, pl.ds(2 * BLOCK, 16), :] = digits
-
-    move_halves = (pl.ds(0, BLOCK), pl.ds(BLOCK, BLOCK + 16))
+            ysend[which, t, d, pl.ds(0, BLOCK), :] = blend(route[which * NY + d], blocks)
+            ysend[which, t, d, pl.ds(BLOCK, 16), :] = digits
+
+    move_halves = (pl.ds(0, BLOCK // 2), pl.ds(BLOCK // 2, YMSG - BLOCK // 2))
     cut_move = lambda ref, part: ref.at[move_halves[part], :]
-    remote("own3", "pair", 2 * BLOCK * BLOCK * 2, ["own"] + mx[1] + mx[3], {"x": pair}, lambda r: (own3.at[0], own3.at[1]))
+    remote("own3", "pair", 2 * BLOCK * BLOCK * 2, ["own"] + mx_first, {"x": pair}, lambda r: (own3.at[0], own3.at[1]))
     for which in range(2):
-        graph.work(("select", which), 0.6, 0, [n for names in mx.values() for n in names], lambda which=which: select(which))
-
-        def merge(own_ref, one, other, which=which):
-            total = own_ref[...].astype(F32) + one[...].astype(F32) + other[...].astype(F32)
-            of = side if which == 0 else 1 - side
-            for t in range(2):
-                z[feature, t, rank_rows(of, MAIN, BLOCK), :] = (
-                    total[t * BLOCK : (t + 1) * BLOCK] + own3[which, t].astype(F32)
-                ).astype(BF16)
-            own_ref[...] = total.astype(BF16)
-
-        ready = [("select", which), "own"] + (["own3"] if which else [])
-        gather_sum(("my", which), "y", YMSG * BLOCK * 2,
-                   lambda j, which=which, ready=ready: ready if j == 0 else [("select", which)],
-                   lambda o, part, which=which: ysend.at[which, o] if part is None else ysend.at[which, o, move_halves[part], :],
-                   0.15, merge, pool_m, cut_move)
+        for t in range(2):
+            tag = (which, t)
+            graph.work(("select", which, t), 0.3, 0, ["route"] + [n for names in mx[t].values() for n in names],
+                       lambda which=which, t=t: select(which, t))
+
+            def merge(own_ref, one, other, which=which, t=t):
+                total = own_ref[...].astype(F32) + one[...].astype(F32) + other[...].astype(F32)
+                of = side if which == 0 else 1 - side
+                z[feature, t, rank_rows(of, MAIN, BLOCK), :] = (total[0:BLOCK] + own3[which, t].astype(F32)).astype(BF16)
+                own_ref[...] = total.astype(BF16)
+
+            ready = [("select", which, t)]
+            gather_sum(("my", which, t), "y", YMSG * BLOCK * 2,
+                       lambda j, which=which, ready=ready: ready + ([] if j else ["own"] + ["own3"] * which),
+                       lambda o, part, which=which, t=t: ysend.at[which, t, o] if part is None
+                       else ysend.at[which, t, o, move_halves[part], :],
+                       0.1, merge, pool_m, cut_move)
 
     def loss_total():
-        digits = ysend[0, y, pl.ds(2 * BLOCK, 16), :].astype(F32)
+        digits = ysend[0, 0, y, pl.ds(BLOCK, 16), :].astype(F32)
         row = lax.broadcasted_iota(jnp.int32, (16, BLOCK), 0) % 3
         parts = jnp.where(row == 0, 256.0 * digits, jnp.where(row == 1, 16.0 * digits, digits))
         return jnp.sum(parts, axis=0, keepdims=True)[:, 0:1]
@@ -406,13 +429,13 @@
     size_a, size_b = ROWS * CUT["a"][1] * 2, ROWS * CUT["b"][1] * 2
     by_own = spread("by", "y", size_b, [], lambda o, part: shard(side, o, x, "b", part))
     by_other = spread("bz", "y", size_b, [], lambda o, part: shard(1 - side, o, x, "b", part))
-    ax = x_spread("ax", size_a, mx[1] + mx[3], mx[1] + mx[3], lambda o, of, part: shard(of, y, o, "a", part))
+    ax = x_spread("ax", size_a, mx_first, mx_first, lambda o, of, part: shard(of, y, o, "a", part), True)
     ay, bx = {}, {}
     for e in ax:
         ay[e] = spread(("ay", e), "y", size_a, ax[e], lambda o, part, e=e: shard(side, o, step("x", -e), "a", part))
     for f in by_own:
-        bx[f] = x_spread(("bx", f), size_b, by_own[f] or mx[1] + mx[3], by_other[f] or mx[1] + mx[3],
-                         lambda o, of, part, f=f: shard(of, step("y", -f), o, "b", part))
+        bx[f] = x_spread(("bx", f), size_b, by_own[f] or mx_first, by_other[f] or mx_first,
+                         lambda o, of, part, f=f: shard(of, step("y", -f), o, "b", part), False)
 
     def hand(name, lo, n, needs):
         def views(receiver):
@@ -421,7 +444,7 @@
 
         remote(name, "pair", 2 * n * BLOCK * 2, needs, {"x": pair}, views)
 
-    hand("pm", 0, MAIN, ["own"] + mx[1] + mx[3])
+    hand("pm", 0, MAIN, ["own"] + mx_first)
     have, turns = {}, []
 
     def turn(c, t, of, lo, n_rows):
@@ -430,7 +453,7 @@
 
     for tag, of, lo, rows, needs in (
         ("zm", side, 0, MAIN, ["own"]), ("zp", 1 - side, 0, MAIN, ["pm"]),
-        ("zl", side, MAIN, BLOCK, [("fin", ("my", 0))]), ("zq", 1 - side, MAIN, BLOCK, [("fin", ("my", 1))]),
+        ("zl", side, MAIN, BLOCK, 0), ("zq", 1 - side, MAIN, BLOCK, 1),
     ):
         have[tag] = []
         for t in range(2):
@@ -441,7 +464,16 @@
                 return z.at[at, t, pl.ds(first, rows // 2), :]
 
             size = rows * BLOCK * 2
-            arrived = spread((tag, t), "z", size, needs, lambda o, part, cut=cut: cut(o * 2 + core, part))
+            begin = needs if lo == 0 else [("fin", ("my", needs, t))]
+            arrived = spread((tag, t), "z", size, begin, lambda o, part, cut=cut: cut(o * 2 + core, part), tag != "zp")
+            if tag == "zp":
+
+                def views(receiver, t=t):
+                    ref = z.at[step("z", NZ // 2) * 2 + core, t, rank_rows(1 - side if receiver else side, 0, MAIN), :]
+                    return ref, ref
+
+                remote((tag, t, "far"), "pair", size, [(("zm", t), "far")], {"x": pair}, views)
+                arrived[NZ // 2] = [(tag, t, "far")]
             shared = ("core", tag, t)
             for g, names in arrived.items():
                 def views(receiver, g=g, cut=cut):
@@ -536,10 +568,7 @@
                 hidden[pl.ds(s * BLOCK, BLOCK), cols] = rows(s) + last * slot_of[s].astype(BF16)
             hidden[pl.ds(MAIN, BLOCK), cols] = last * stays.astype(BF16)
 
-    hidden_copy = pltpu.make_async_copy(hidden, hidden_out, own_sem.at[8])
-    sums_copy = pltpu.make_async_copy(sums_out, sums_hbm, own_sem.at[9])
     graph.work("store hidden", 0.3, 9, [("hidden", i) for i in range(WORK)], store_hidden)
-    graph.work("send hidden", 0.0, 9, ["store hidden"], hidden_copy.start)
 
     def backward(j):
         rows = pl.ds(pl.multiple_of(step("y", j) * 256, 256), 256)
@@ -605,28 +634,24 @@
             mates.append(copy)
         else:
             node[4](True).wait_recv()
-    sums_copy.start()
     for mates in started.values():
         for copy in mates[-RING:]:
             copy.wait_send()
-    hidden_copy.wait()
-    sums_copy.wait()
-    assert len(index) == RECEIVES
-
-
-RECEIVES = 278
+    assert len(index) == RECEIVES, len(index)
+
+
+RECEIVES = 244
 
 
 def big(counts, moves, seg, tok, grad, gate, up, down):
-    vmem, smem = pl.BlockSpec(memory_space=pltpu.VMEM), pl.BlockSpec(memory_space=pltpu.SMEM)
-    anyw = pl.BlockSpec(memory_space=pl.ANY)
+    anyw, hbm = pl.BlockSpec(memory_space=pl.ANY), pl.BlockSpec(memory_space=pltpu.HBM)
     width = NX * NY * ROWS
     wide_a, wide_b = CUT["a"][1], CUT["b"][1]
     return pl.pallas_call(
         big_kernel,
-        out_shape=(jax.ShapeDtypeStruct((RANK, HID), BF16), jax.ShapeDtypeStruct((2, ROWS, COLS), F32)),
-        in_specs=[smem, smem, vmem] + [anyw] * 5,
-        out_specs=(anyw,) * 2,
+        out_shape=(pltpu.VMEM((RANK, HID), BF16), pltpu.VMEM((2, ROWS, COLS), F32)),
+        in_specs=[hbm] * 8,
+        out_specs=(pl.BlockSpec(memory_space=pltpu.VMEM),) * 2,
         scratch_shapes=[
             pltpu.VMEM((2, width, COLS), BF16),
             pltpu.VMEM((2 * NZ, 2, 2 * RANK, BLOCK), BF16),
@@ -639,19 +664,20 @@
             pltpu.VMEM((NY + 1, 2, ROWS, wide_b), BF16),
             pltpu.VMEM((NY + 1, 4, ROWS // 2, wide_b), BF16),
             pltpu.VMEM((16, ROWS, wide_b), BF16),
-            pltpu.VMEM((16, YMSG, BLOCK), BF16),
-            pltpu.VMEM((NX * MSG, BLOCK), BF16),
-            pltpu.VMEM((2, NY, YMSG, BLOCK), BF16),
+            pltpu.VMEM((32, YMSG, BLOCK), BF16),
+            pltpu.VMEM((2, NX, MSG, BLOCK), BF16),
+            pltpu.VMEM((2, 2, NY, YMSG, BLOCK), BF16),
             pltpu.VMEM((2, 2, BLOCK, BLOCK), BF16),
             pltpu.VMEM((CAP * BLOCK, BLOCK), BF16),
             pltpu.VMEM((CAP * BLOCK, BLOCK), BF16),
             pltpu.VMEM((BLOCK, BLOCK), F32),
             pltpu.VMEM((RANK, PART), BF16),
-            pltpu.VMEM((RANK, HID), BF16),
-            pltpu.VMEM((2, ROWS, COLS), F32),
+            pltpu.SMEM((1,), jnp.int32),
+            pltpu.SMEM((3, MOVES), jnp.int32),
+            pltpu.VMEM((CAP, BLOCK), jnp.int32),
             pltpu.SemaphoreType.DMA((RING * len(LINKS),)),
             pltpu.SemaphoreType.DMA((RECEIVES,)),
-            pltpu.SemaphoreType.DMA((10,)),
+            pltpu.SemaphoreType.DMA((11,)),
         ],
         compiler_params=pltpu.CompilerParams(
             collective_id=0, has_side_effects=True, vmem_limit_bytes=60 * 1024 * 1024
@@ -659,34 +685,20 @@
     )(counts, moves, seg, tok, grad, gate, up, down)
 
 
-def finish_kernel(hidden_in, sums, hidden, gate_out, up_out, down_out, rows, grads, sems):
+def finish_kernel(hidden_in, sums, hidden, gate_out, up_out, down_out, sems):
     quarter = RANK // 4
-    ins = [
-        pltpu.make_async_copy(hidden_in.at[pl.ds(i * quarter, quarter), :], rows.at[pl.ds(i * quarter, quarter), :], sems.at[i])
+    copies = [
+        pltpu.make_async_copy(hidden_in.at[pl.ds(i * quarter, quarter), :], hidden.at[pl.ds(i * quarter, quarter), :], sems.at[i])
         for i in range(4)
     ]
-    ins += [
-        pltpu.make_async_copy(
-            sums.at[p, :, pl.ds(i * PART, PART)], grads.at[i, :, pl.ds(p * PART, PART)], sems.at[4 + 2 * i + p]
-        )
-        for i in range(3)
+    copies += [
+        pltpu.make_async_copy(sums.at[p, :, pl.ds(i * PART, PART)], out.at[:, pl.ds(p * PART, PART)], sems.at[4 + 2 * i + p])
+        for i, out in enumerate((gate_out, up_out, down_out))
         for p in range(2)
     ]
-    outs = [
-        pltpu.make_async_copy(rows.at[pl.ds(i * quarter, quarter), :], hidden.at[pl.ds(i * quarter, quarter), :], sems.at[10 + i])
-        for i in range(4)
-    ]
-    outs += [pltpu.make_async_copy(grads.at[i], ref, sems.at[14 + i]) for i, ref in enumerate((gate_out, up_out, down_out))]
-    for copy in ins:
+    for copy in copies:
         copy.start()
-    for i in range(4):
-        ins[i].wait()
-        outs[i].start()
-    for i in range(3):
-        ins[4 + 2 * i].wait()
-        ins[5 + 2 * i].wait()
-        outs[4 + i].start()
-    for copy in outs:
+    for copy in copies:
         copy.wait()
 
 
@@ -697,12 +709,9 @@
         finish_kernel,
         out_shape=(jax.ShapeDtypeStruct(hidden.shape, BF16), grad, grad, grad),
         in_specs=[anyw] * 2,
-        out_specs=(anyw,) * 4,
-        scratch_shapes=[
-            pltpu.VMEM(hidden.shape, BF16),
-            pltpu.VMEM((3, ROWS, HID), F32),
-            pltpu.SemaphoreType.DMA((17,)),
-        ],
+        out_specs=(pl.BlockSpec(memory_space=pltpu.HBM),) * 4,
+        scratch_shapes=[pltpu.SemaphoreType.DMA((10,))],
+        compiler_params=pltpu.CompilerParams(vmem_limit_bytes=1024 * 1024),
     )(hidden, sums)
 
 

time: 98.9 us -> 93.9 us (0.949)
  Pallas kernels: 97.3 us -> 92.2 us
    pallas_call x1, Pallas kernels: 95.2 us -> 91.2 us  [big(): pl.pallas_call(big_kernel, out_shape=(pltpu.VMEM((RANK, HID), BF16), pltp...]
    pallas_call x1, Pallas kernels: 2.03 us -> 1 us  [finish(): pl.pallas_call(finish_kernel, out_shape=(jax.ShapeDtypeStruct(hidden.shap...]
where the time goes in v4:
time: 93.9 us; the launch traced here: 93.6 us
  Pallas kernels  92.2 us (98%)
  between operations  1.45 us (2%)
    pallas_call x1, Pallas kernels, big(): pl.pallas_call(big_kernel, out_shape=(pltpu.VMEM((RANK, HID), BF16), pltp...  91.2 us

profile of v4, /device:TPU:1, one launch (start us, length us, event | category | flops | bytes accessed | tf_op | source)
XLA Modules:
  0.0 93.6 jit_solution(13013356814679315787)
XLA Ops:
  1.3 91.2 %shard_map.111 = (bf16[512,512]{1,0:T(8,128)(2,1)S(1)}, f32[2,64,768]{2,1,0:T(8,128)S(1)}) custom-call(s32[1]{0:T(128)S(6)} %copy.12.counts_hbm, s32[3,16]{1,0:T(4,128)} %bitcast.3, s32[6,128]{1,0:T(8,128)} %bitcast.2, bf16[768,128]{1,0:T(8,128)(2,1)} %tok.1, bf16[768,128]{1,0:T(8,128)(2,1)} %grad.1, bf16[64,512]{1,0:T(8,128)(2,1)} %gate.1, ...), custom_call_target="tpu_custom_call" | custom-call | tf_op jit(solution)/shard_map/pallas_call | solution.py:650
  92.5 1.0 %shard_map.112 = (bf16[512,512]{1,0:T(8,128)(2,1)}, f32[64,512]{1,0:T(8,128)}, f32[64,512]{1,0:T(8,128)}, f32[64,512]{1,0:T(8,128)}) custom-call(bf16[512,512]{1,0:T(8,128)(2,1)S(1)} %get-tuple-element.6.hidden_in, f32[2,64,768]{2,1,0:T(8,128)S(1)} %get-tuple-element.7.sums), custom_call_target="tpu_custom_call" | custom-call | tf_op jit(solution)/shard_map/pallas_call | solution.py:708

commit v5 on v4

--- a/solution.py
+++ b/solution.py
@@ -22,7 +22,9 @@
 MSG = 2 * BLOCK + 16
 YMSG = BLOCK + 16
 CUT = {"a": (0, 384), "b": (384, 384)}
+LOAD = {"a": (0, 512), "b": (512, 256)}
 LINKS = ("x+", "x-", "y+", "y-", "z+", "z-", "core", "pair")
+PAIRED = (2, 3)
 RING = 4
 MESH = pl.DeviceIdType.MESH
 BF16, F32 = jnp.bfloat16, jnp.float32
@@ -56,7 +58,7 @@
     return stay, leave, slot
 
 
-def routes(y, columns, moves):
+def routes(y, x, moves):
     zero, one = jnp.int32(0), jnp.int32(1)
     src = [moves[0, m] for m in range(MOVES)]
     dst = [moves[1, m] for m in range(MOVES)]
@@ -68,12 +70,11 @@
         here = (src[m] >= y * NX) & (src[m] < y * NX + NX)
         number.append(jnp.where(here, (src[m] - y * NX) * 2 + second, -one))
     result = []
-    for to_x in columns:
-        for d in range(NY):
-            at = -one
-            for m in range(MOVES):
-                at = jnp.where(dst[m] == d * NX + to_x, number[m], at)
-            result.append([factor(at == i) for i in range(2 * NX)])
+    for d in range(NY):
+        at = -one
+        for m in range(MOVES):
+            at = jnp.where(dst[m] == d * NX + x, number[m], at)
+        result.append([factor(at == i) for i in range(2 * NX)])
     return result
 
 
@@ -96,7 +97,7 @@
         self.nodes[name] = ("work", cost, rank, tuple(needs), run)
 
     rate, lag = 46.6e3, 2.5
-    early, late, along_z = 0.6, 1.0, 1.0
+    early, late, along_z = 0.8, 1.0, 1.0
     seed, noise = 0, 0.0
 
     def span(self, n):
@@ -124,7 +125,7 @@
         todo = sorted(nodes, key=lambda n: -moved[n])
         done, flying, free, now, steps, times = set(), [], {}, 0.0, [], {}
         while todo or flying:
-            landed = ("fin", ("my", 1, 1)) in done
+            landed = ("pl", 1) in done
             for name in [n for n in todo if nodes[n][0] == "send"]:
                 _, link, size, needs = nodes[name][:4]
                 ways = ("x+", "x-") if link == "pair" else (link,)
@@ -224,24 +225,27 @@
 
         graph.work(shared, 0.0, 0, members, wait)
 
-    def spread(tag, axis, size, needs, piece, to_far=True):
+    def spread(tag, axis, size, needs, piece, hops=None):
         n = size_of[axis]
         arrived = {0: list(needs)}
         far = (tag, "far")
-        for hop in range(1, n // 2 + to_far):
+        hops = n // 2 if hops is None else hops
+        for hop in range(1, hops + 1):
+            base = hop - 1
             for sign in (1, -1):
                 part = None if hop < n // 2 else (0 if sign > 0 else 1)
 
-                def views(receiver, sign=sign, hop=hop, part=part):
-                    ref = piece(step(axis, -sign * (hop if receiver else hop - 1)), part)
+                def views(receiver, sign=sign, hop=hop, base=base, part=part):
+                    ref = piece(step(axis, -sign * (hop if receiver else base)), part)
                     return ref, ref
 
-                remote((tag, sign, hop), axis + "-+"[sign > 0], size if part is None else size // 2,
-                       needs if hop == 1 else [(tag, sign, hop - 1)], {axis: step(axis, sign)}, views,
+                share = size if part is None else size // 2
+                remote((tag, sign, hop), axis + "-+"[sign > 0], share * (hop - base),
+                       [(tag, sign, base)] if base else needs, {axis: step(axis, sign * (hop - base))}, views,
                        None if part is None else far)
                 if part is None:
                     arrived[sign * hop % n] = [(tag, sign, hop)]
-        if to_far:
+        if hops == n // 2:
             join(far, [(tag, 1, n // 2), (tag, -1, n // 2)], lambda: piece(step(axis, n // 2), None))
             arrived[n // 2] = [far]
         return arrived
@@ -267,9 +271,10 @@
             remote((tag, sign, 0), "x" + "-+"[sign > 0], size, other_needs, {"x": step("x", sign)}, other,
                    None if forwarded else far)
         if forwarded:
-            join(far, [(tag, 1, 2), (tag, -1, 2)], lambda: slots_a.at[0])
+            join(far, [(tag, 1, 2), (tag, -1, 2)], lambda: w.at[0, pl.ds(0, ROWS), pl.ds(*LOAD["a"])])
             return {0: list(needs), 1: [(tag, 1, 0)], 3: [(tag, -1, 0)], 2: [far]}
-        join(far, [(tag, sign, hop) for sign in (1, -1) for hop in (0, 2)], lambda: slots_a.at[pl.ds(0, 3)])
+        join(far, [(tag, sign, hop) for sign in (1, -1) for hop in (0, 2)],
+             lambda: w.at[0, pl.ds(0, 3 * ROWS), pl.ds(*LOAD["b"])])
         return {0: list(needs), 1: [far], 3: [far], 2: [far]}
 
     def gather_sum(tag, axis, size, own_ready, piece, cost, finish, pool, halves):
@@ -370,11 +375,11 @@
                 if s < WORK - 1:
                     z[feature, t, rank_rows(side, s * BLOCK, BLOCK), :] = rows
                 else:
-                    own3[0, t] = rows
+                    own3[t] = rows
 
     graph.work("own", 0.3, 0, [], prepare_own)
 
-    graph.work("route", 0.5, 0, [], lambda: route.extend(routes(y, (x, pair), moves)))
+    graph.work("route", 0.5, 0, [], lambda: route.extend(routes(y, x, moves)))
     mx = []
     for t in range(2):
         def message(o, part, t=t):
@@ -384,37 +389,35 @@
         mx.append(spread(("mx", t), "x", MSG * BLOCK * 2, [], message))
     mx_first = mx[0][1] + mx[0][3] + mx[1][1] + mx[1][3]
 
-    def select(which, t):
+    def select(t):
         digits = sum(xbuf[t, i, pl.ds(2 * BLOCK, 16), :].astype(F32) for i in range(NX)).astype(BF16)
         blocks = [xbuf[t, i // 2, pl.ds(i % 2 * BLOCK, BLOCK), :] for i in range(2 * NX)]
         for d in range(NY):
-            ysend[which, t, d, pl.ds(0, BLOCK), :] = blend(route[which * NY + d], blocks)
-            ysend[which, t, d, pl.ds(BLOCK, 16), :] = digits
+            ysend[t, d, pl.ds(0, BLOCK), :] = blend(route[d], blocks)
+            ysend[t, d, pl.ds(BLOCK, 16), :] = digits
 
     move_halves = (pl.ds(0, BLOCK // 2), pl.ds(BLOCK // 2, YMSG - BLOCK // 2))
     cut_move = lambda ref, part: ref.at[move_halves[part], :]
-    remote("own3", "pair", 2 * BLOCK * BLOCK * 2, ["own"] + mx_first, {"x": pair}, lambda r: (own3.at[0], own3.at[1]))
-    for which in range(2):
-        for t in range(2):
-            tag = (which, t)
-            graph.work(("select", which, t), 0.3, 0, ["route"] + [n for names in mx[t].values() for n in names],
-                       lambda which=which, t=t: select(which, t))
-
-            def merge(own_ref, one, other, which=which, t=t):
-                total = own_ref[...].astype(F32) + one[...].astype(F32) + other[...].astype(F32)
-                of = side if which == 0 else 1 - side
-                z[feature, t, rank_rows(of, MAIN, BLOCK), :] = (total[0:BLOCK] + own3[which, t].astype(F32)).astype(BF16)
-                own_ref[...] = total.astype(BF16)
-
-            ready = [("select", which, t)]
-            gather_sum(("my", which, t), "y", YMSG * BLOCK * 2,
-                       lambda j, which=which, ready=ready: ready + ([] if j else ["own"] + ["own3"] * which),
-                       lambda o, part, which=which, t=t: ysend.at[which, t, o] if part is None
-                       else ysend.at[which, t, o, move_halves[part], :],
-                       0.1, merge, pool_m, cut_move)
+    for t in range(2):
+        graph.work(("select", t), 0.3, 0, ["route"] + [n for names in mx[t].values() for n in names], lambda t=t: select(t))
+
+        def merge(own_ref, one, other, t=t):
+            total = own_ref[...].astype(F32) + one[...].astype(F32) + other[...].astype(F32)
+            z[feature, t, rank_rows(side, MAIN, BLOCK), :] = (total[0:BLOCK] + own3[t].astype(F32)).astype(BF16)
+            own_ref[...] = total.astype(BF16)
+
+        gather_sum(("my", t), "y", YMSG * BLOCK * 2, lambda j, t=t: [("select", t)] + ([] if j else ["own"]),
+                   lambda o, part, t=t: ysend.at[t, o] if part is None else ysend.at[t, o, move_halves[part], :],
+                   0.1, merge, pool_m, cut_move)
+
+        def handed(receiver, t=t):
+            ref = z.at[feature, t, rank_rows(1 - side if receiver else side, MAIN, BLOCK), :]
+            return ref, ref
+
+        remote(("pl", t), "pair", BLOCK * BLOCK * 2, [("fin", ("my", t))], {"x": pair}, handed)
 
     def loss_total():
-        digits = ysend[0, 0, y, pl.ds(BLOCK, 16), :].astype(F32)
+        digits = ysend[0, y, pl.ds(BLOCK, 16), :].astype(F32)
         row = lax.broadcasted_iota(jnp.int32, (16, BLOCK), 0) % 3
         parts = jnp.where(row == 0, 256.0 * digits, jnp.where(row == 1, 16.0 * digits, digits))
         return jnp.sum(parts, axis=0, keepdims=True)[:, 0:1]
@@ -424,17 +427,17 @@
         return pl.ds(first, ROWS if part is None else 32)
 
     def shard(of, at_y, at_x, cut, part):
-        return w.at[of, shard_rows(at_y, at_x, part), pl.ds(*CUT[cut])]
-
-    size_a, size_b = ROWS * CUT["a"][1] * 2, ROWS * CUT["b"][1] * 2
-    by_own = spread("by", "y", size_b, [], lambda o, part: shard(side, o, x, "b", part))
-    by_other = spread("bz", "y", size_b, [], lambda o, part: shard(1 - side, o, x, "b", part))
-    ax = x_spread("ax", size_a, mx_first, mx_first, lambda o, of, part: shard(of, y, o, "a", part), True)
+        return w.at[of, shard_rows(at_y, at_x, part), pl.ds(*LOAD[cut])]
+
+    load_a, load_b = (ROWS * LOAD[cut][1] * 2 for cut in "ab")
+    by_own = spread("by", "y", load_b, [], lambda o, part: shard(side, o, x, "b", part))
+    by_other = spread("bz", "y", load_b, [], lambda o, part: shard(1 - side, o, x, "b", part))
+    ax = x_spread("ax", load_a, mx_first, mx_first, lambda o, of, part: shard(of, y, o, "a", part), True)
     ay, bx = {}, {}
     for e in ax:
-        ay[e] = spread(("ay", e), "y", size_a, ax[e], lambda o, part, e=e: shard(side, o, step("x", -e), "a", part))
+        ay[e] = spread(("ay", e), "y", load_a, ax[e], lambda o, part, e=e: shard(side, o, step("x", -e), "a", part))
     for f in by_own:
-        bx[f] = x_spread(("bx", f), size_b, by_own[f] or mx_first, by_other[f] or mx_first,
+        bx[f] = x_spread(("bx", f), load_b, by_own[f] or mx_first, by_other[f] or mx_first,
                          lambda o, of, part, f=f: shard(of, step("y", -f), o, "b", part), False)
 
     def hand(name, lo, n, needs):
@@ -445,7 +448,7 @@
         remote(name, "pair", 2 * n * BLOCK * 2, needs, {"x": pair}, views)
 
     hand("pm", 0, MAIN, ["own"] + mx_first)
-    have, turns = {}, []
+    have, turns, landed_of = {}, [], {}
 
     def turn(c, t, of, lo, n_rows):
         rows = rank_rows(of, lo, n_rows)
@@ -453,7 +456,7 @@
 
     for tag, of, lo, rows, needs in (
         ("zm", side, 0, MAIN, ["own"]), ("zp", 1 - side, 0, MAIN, ["pm"]),
-        ("zl", side, MAIN, BLOCK, 0), ("zq", 1 - side, MAIN, BLOCK, 1),
+        ("zl", side, MAIN, BLOCK, []), ("zq", 1 - side, MAIN, BLOCK, []),
     ):
         have[tag] = []
         for t in range(2):
@@ -464,16 +467,18 @@
                 return z.at[at, t, pl.ds(first, rows // 2), :]
 
             size = rows * BLOCK * 2
-            begin = needs if lo == 0 else [("fin", ("my", needs, t))]
-            arrived = spread((tag, t), "z", size, begin, lambda o, part, cut=cut: cut(o * 2 + core, part), tag != "zp")
-            if tag == "zp":
-
-                def views(receiver, t=t):
-                    ref = z.at[step("z", NZ // 2) * 2 + core, t, rank_rows(1 - side if receiver else side, 0, MAIN), :]
+            begin = {"zl": [("fin", ("my", t))], "zq": [("pl", t)]}.get(tag, needs)
+            hops = PAIRED[t] if tag == "zp" else NZ // 2
+            arrived = spread((tag, t), "z", size, begin, lambda o, part, cut=cut: cut(o * 2 + core, part), hops)
+            landed_of[tag, t] = arrived
+            for g in range(hops + 1, NZ - hops):
+
+                def views(receiver, t=t, g=g):
+                    ref = z.at[step("z", -g) * 2 + core, t, rank_rows(1 - side if receiver else side, 0, MAIN), :]
                     return ref, ref
 
-                remote((tag, t, "far"), "pair", size, [(("zm", t), "far")], {"x": pair}, views)
-                arrived[NZ // 2] = [(tag, t, "far")]
+                remote((tag, t, g), "pair", size, landed_of["zm", t][g], {"x": pair}, views)
+                arrived[g] = [(tag, t, g)]
             shared = ("core", tag, t)
             for g, names in arrived.items():
                 def views(receiver, g=g, cut=cut):
@@ -490,7 +495,6 @@
                     graph.work(turns[-1], 0.1 if lo == 0 else 0.04, 3, [shared] if far else names,
                                lambda g=g, far=far, t=t, of=of, lo=lo, rows=rows: turn(
                                    step("z", -g) * 2 + (1 - core if far else core), t, of, lo, rows))
-    last_needs = have["zl"] + have["zq"]
 
     seen = []
 
@@ -506,22 +510,12 @@
             new = jnp.dot(left, w[side, rows, cols], preferred_element_type=F32)
             acc[slots, cols] = new if start else acc[slots, cols] + new
 
-    last_rows = [pl.ds(p * RANK + MAIN, BLOCK) for p in range(2)]
-
-    def forward_last():
-        for t, lo, hi in ((0, 0, 2), (1, 2, 3)):
-            left = jnp.concatenate(
-                [jnp.concatenate([z[c, t, slots, :] for c in range(2 * NZ)], axis=1) for slots in last_rows], axis=0
-            )
-
-            def tile(n, _, left=left):
-                cols = pl.ds(pl.multiple_of(n * PART, PART), PART)
-                new = jnp.dot(left, w[side, :, cols], preferred_element_type=F32)
-                for p, slots in enumerate(last_rows):
-                    acc[slots, cols] = new[p * BLOCK : (p + 1) * BLOCK]
-                return 0
-
-            lax.fori_loop(lo, hi, tile, 0)
+    def forward_last(of):
+        slots = rank_rows(of, MAIN, BLOCK)
+        for t, lo, n in ((0, 0, 2 * PART), (1, 2 * PART, PART)):
+            left = jnp.concatenate([z[c, t, slots, :] for c in range(2 * NZ)], axis=1)
+            cols = pl.ds(lo, n)
+            acc[slots, cols] = jnp.dot(left, w[side, :, cols], preferred_element_type=F32)
 
     all_landed = []
     for f in range(NY):
@@ -529,11 +523,12 @@
         all_landed += landed
         for tag, of in (("zm", side), ("zp", 1 - side)):
             graph.work(("fwd", tag, f), 0.6, 2, have[tag] + landed, lambda f=f, tag=tag, of=of: forward(f, tag, of))
-    graph.work("fwd last", 1.3, 2, last_needs + all_landed, forward_last)
-
-    def pointwise():
+    for tag, of in (("zl", side), ("zq", 1 - side)):
+        graph.work(("fwd last", tag), 0.8, 2, have[tag] + all_landed, lambda of=of: forward_last(of))
+
+    def pointwise(of, lo, n):
         def rows_of(i, _):
-            rows = pl.ds(pl.multiple_of(i * 64, 64), 64)
+            rows = pl.ds(pl.multiple_of(of * RANK + lo + i * 64, 64), 64)
             g, u, b = acc[rows, 0:PART], acc[rows, PART : 2 * PART], acc[rows, 2 * PART : COLS]
             logistic = jax.nn.sigmoid(g)
             activated = g * logistic
@@ -542,9 +537,13 @@
             act[rows, 2 * PART : COLS] = (activated * u).astype(BF16)
             return 0
 
-        lax.fori_loop(0, 16, rows_of, 0)
-
-    graph.work("pointwise", 0.6, 2, [("fwd", tag, f) for tag in ("zm", "zp") for f in range(NY)] + ["fwd last"] + turns, pointwise)
+        lax.fori_loop(0, n // 64, rows_of, 0)
+
+    for tag, of in (("zm", side), ("zp", 1 - side)):
+        graph.work(("pointwise", tag), 0.25, 2, [("fwd", tag, f) for f in range(NY)], lambda of=of: pointwise(of, 0, MAIN))
+    for tag, of in (("zl", side), ("zq", 1 - side)):
+        graph.work(("pointwise", tag), 0.1, 2, [("fwd last", tag)], lambda of=of: pointwise(of, MAIN, BLOCK))
+    graph.work("pointwise", 0.0, 2, [("pointwise", tag) for tag in have] + turns, lambda: None)
 
     for i in range(WORK):
         def views(receiver, i=i):
@@ -578,6 +577,8 @@
 
     for i, j in enumerate((4, 5, 3, 6, 2, 7, 1, 0)):
         graph.work(("bwd", j), 0.9, 1 + i, ["pointwise"], lambda j=j: backward(j))
+
+    size_a, size_b = (ROWS * CUT[cut][1] * 2 for cut in "ab")
 
     def plain(own_ref, one, other):
         own_ref[...] = (own_ref[...].astype(F32) + one[...].astype(F32) + other[...].astype(F32)).astype(BF16)
@@ -637,10 +638,10 @@
     for mates in started.values():
         for copy in mates[-RING:]:
             copy.wait_send()
-    assert len(index) == RECEIVES, len(index)
-
-
-RECEIVES = 244
+    assert len(index) == RECEIVES
+
+
+RECEIVES = 231
 
 
 def big(counts, moves, seg, tok, grad, gate, up, down):
@@ -664,10 +665,10 @@
             pltpu.VMEM((NY + 1, 2, ROWS, wide_b), BF16),
             pltpu.VMEM((NY + 1, 4, ROWS // 2, wide_b), BF16),
             pltpu.VMEM((16, ROWS, wide_b), BF16),
-            pltpu.VMEM((32, YMSG, BLOCK), BF16),
+            pltpu.VMEM((16, YMSG, BLOCK), BF16),
             pltpu.VMEM((2, NX, MSG, BLOCK), BF16),
-            pltpu.VMEM((2, 2, NY, YMSG, BLOCK), BF16),
-            pltpu.VMEM((2, 2, BLOCK, BLOCK), BF16),
+            pltpu.VMEM((2, NY, YMSG, BLOCK), BF16),
+            pltpu.VMEM((2, BLOCK, BLOCK), BF16),
             pltpu.VMEM((CAP * BLOCK, BLOCK), BF16),
             pltpu.VMEM((CAP * BLOCK, BLOCK), BF16),
             pltpu.VMEM((BLOCK, BLOCK), F32),

time: 93.9 us -> 92.4 us (0.984)
  Pallas kernels: 92.2 us -> 90.8 us
    pallas_call x1, Pallas kernels: 91.2 us -> 89.8 us  [big(): pl.pallas_call(big_kernel, out_shape=(pltpu.VMEM((RANK, HID), BF16), pltp...]
where the time goes in v5:
time: 92.4 us; the launch traced here: 92.3 us
  Pallas kernels  90.8 us (98%)
  between operations  1.45 us (2%)
    pallas_call x1, Pallas kernels, big(): pl.pallas_call(big_kernel, out_shape=(pltpu.VMEM((RANK, HID), BF16), pltp...  89.8 us

profile of v5, /device:TPU:1, one launch (start us, length us, event | category | flops | bytes accessed | tf_op | source)
XLA Modules:
  0.0 92.3 jit_solution(16135599121909381181)
XLA Ops:
  1.3 89.8 %shard_map.111 = (bf16[512,512]{1,0:T(8,128)(2,1)S(1)}, f32[2,64,768]{2,1,0:T(8,128)S(1)}) custom-call(s32[1]{0:T(128)S(6)} %copy.12.counts_hbm, s32[3,16]{1,0:T(4,128)} %bitcast.3, s32[6,128]{1,0:T(8,128)} %bitcast.2, bf16[768,128]{1,0:T(8,128)(2,1)} %tok.1, bf16[768,128]{1,0:T(8,128)(2,1)} %grad.1, bf16[64,512]{1,0:T(8,128)(2,1)} %gate.1, ...), custom_call_target="tpu_custom_call" | custom-call | tf_op jit(solution)/shard_map/pallas_call | solution.py:651
  91.1 1.0 %shard_map.112 = (bf16[512,512]{1,0:T(8,128)(2,1)}, f32[64,512]{1,0:T(8,128)}, f32[64,512]{1,0:T(8,128)}, f32[64,512]{1,0:T(8,128)}) custom-call(bf16[512,512]{1,0:T(8,128)(2,1)S(1)} %get-tuple-element.6.hidden_in, f32[2,64,768]{2,1,0:T(8,128)S(1)} %get-tuple-element.7.sums), custom_call_target="tpu_custom_call" | custom-call | tf_op jit(solution)/shard_map/pallas_call | solution.py:709

commit v6 on v5

--- a/solution.py
+++ b/solution.py
@@ -569,14 +569,21 @@
 
     graph.work("store hidden", 0.3, 9, [("hidden", i) for i in range(WORK)], store_hidden)
 
-    def backward(j):
+    def backward(j, spans):
         rows = pl.ds(pl.multiple_of(step("y", j) * 256, 256), 256)
-        for t, lo, n in ((0, 0, 2 * PART), (1, 2 * PART, PART)):
+        for t, lo, n in spans:
             cols = pl.ds(lo, n)
             tb[rows, cols] = jnp.dot(xt[t, rows, :], act[:, cols], preferred_element_type=F32).astype(BF16)
 
-    for i, j in enumerate((4, 5, 3, 6, 2, 7, 1, 0)):
-        graph.work(("bwd", j), 0.9, 1 + i, ["pointwise"], lambda j=j: backward(j))
+    first_b, edge = CUT["b"][0], 2 * PART
+    graph.work(("bwd", 4, "b"), 0.45, 0, ["pointwise"],
+               lambda: backward(4, ((0, first_b, edge - first_b), (1, edge, COLS - edge))))
+    graph.work(("bwd", 4, "a"), 0.4, 0, ["pointwise", ("bwd", 4, "b")], lambda: backward(4, ((0, 0, first_b),)))
+    for i, j in enumerate((5, 3, 6, 2, 7, 1, 0)):
+        graph.work(("bwd", j), 0.8, 1 + i, ["pointwise"], lambda j=j: backward(j, ((0, 0, edge), (1, edge, PART))))
+
+    def done_of(j, cut):
+        return [("bwd", j, cut)] if j == 4 else [("bwd", j)]
 
     size_a, size_b = (ROWS * CUT[cut][1] * 2 for cut in "ab")
 
@@ -599,7 +606,7 @@
 
     row_halves = (pl.ds(0, 32), pl.ds(32, 32))
     for e in (2, 1, 3, 0):
-        gather_sum(("say", e), "y", size_a, lambda j: [("bwd", j)],
+        gather_sum(("say", e), "y", size_a, lambda j: done_of(j, "a"),
                    lambda o, part, e=e: term(o, step("x", e), "a", part), 0.1, plain, pool_a,
                    lambda ref, part: ref.at[row_halves[part], :])
     for f in (4, 5, 3, 6, 2, 7, 1, 0):
@@ -608,7 +615,7 @@
             tb2[at, side] = same.astype(BF16)
             tb2[at, 1 - side] = other.astype(BF16)
 
-        x_sum(("sbx", f), size_b, lambda e, f=f: [("bwd", f)],
+        x_sum(("sbx", f), size_b, lambda e, f=f: done_of(f, "b"),
               lambda o, part, f=f: term(step("y", f), o, "b", part), keep, f)
     x_sum("sax", size_a, lambda e: [("fin", ("say", e))], lambda o, part: term(y, o, "a", part), final_a, NY)
 

time: 92.4 us -> 93.3 us (level)
  no operation moved by 1% of the time
where the time goes in v6:
time: 93.3 us; the launch traced here: 93.2 us
  Pallas kernels  91.7 us (98%)
  between operations  1.45 us (2%)
    pallas_call x1, Pallas kernels, big(): pl.pallas_call(big_kernel, out_shape=(pltpu.VMEM((RANK, HID), BF16), pltp...  90.7 us

profile of v6, /device:TPU:1, one launch (start us, length us, event | category | flops | bytes accessed | tf_op | source)
XLA Modules:
  0.0 93.2 jit_solution(9827357545142360229)
XLA Ops:
  1.3 90.7 %shard_map.111 = (bf16[512,512]{1,0:T(8,128)(2,1)S(1)}, f32[2,64,768]{2,1,0:T(8,128)S(1)}) custom-call(s32[1]{0:T(128)S(6)} %copy.12.counts_hbm, s32[3,16]{1,0:T(4,128)} %bitcast.3, s32[6,128]{1,0:T(8,128)} %bitcast.2, bf16[768,128]{1,0:T(8,128)(2,1)} %tok.1, bf16[768,128]{1,0:T(8,128)(2,1)} %grad.1, bf16[64,512]{1,0:T(8,128)(2,1)} %gate.1, ...), custom_call_target="tpu_custom_call" | custom-call | tf_op jit(solution)/shard_map/pallas_call | solution.py:658
  92.0 1.0 %shard_map.112 = (bf16[512,512]{1,0:T(8,128)(2,1)}, f32[64,512]{1,0:T(8,128)}, f32[64,512]{1,0:T(8,128)}, f32[64,512]{1,0:T(8,128)}) custom-call(bf16[512,512]{1,0:T(8,128)(2,1)S(1)} %get-tuple-element.6.hidden_in, f32[2,64,768]{2,1,0:T(8,128)S(1)} %get-tuple-element.7.sums), custom_call_target="tpu_custom_call" | custom-call | tf_op jit(solution)/shard_map/pallas_call | solution.py:716
